TPU v7x, 32 devices: a whole 2x2x4 slice. The times are simulated.
32 devices in a mesh: ens: 2 (over y), gx: 4 (over z), col: 2 (over x), gz: 2 (over core).
Axes of the slice: x: 2, y: 2, z: 4, core: 2. Of those that a mesh axis runs over, the one named last changes fastest.
Arguments:
- checkpoints: bfloat16 [8, 3, 32, 8, 256], P(('ens', 'col'), None, 'gz', 'gx'), parts along dimension 0, may hold values from -3 to 3
- obs_values: float32 [8, 32, 8, 256], P('ens', 'gz', 'gx', 'col'), parts along dimension 0, may hold values from -3 to 3
- obs_mask: int32 [8, 32, 8, 256], P('ens', 'gz', 'gx', 'col'), parts along dimension 0, may hold values 0 or 1
- drag: float32 [64], P(('ens', 'gz')), parts along dimension 0, may hold values from 0.05 to 0.5
Outputs:
- grad_init: float32 [6, 32, 8, 256], P('ens', 'gz', 'gx', 'col'), parts along dimension 0
- cost_levels: float32 [64], P(('ens', 'gz')), parts along dimension 0
- drag_grad: float32 [64], P(('ens', 'gz')), parts along dimension 0
There are 2 independent parts, one for each index of `ens`. A program takes and returns all parts, laid end to end along the dimension named above; each array names one. Nothing has to cross between parts.
All inputs are finite; a program needn't handle non-finite values. No bound on the sum of `obs_mask` on one device may be relied on, other than what follows from the above.
Results may differ from a plain program's by a relative error of at most 0.0003.
Values may be sent and summed in bfloat16 or wider, within the bound.
A program may use at most 64 MiB of HBM per device.

v0:
```python
import jax
import jax.numpy as jnp
from jax import lax
from jax.sharding import PartitionSpec as P

SEG = 2
time_step = 0.1
viscosity = 0.05
vertical_mix = 0.2


def with_halo(x, sides, width):
    for axis, dim in sides:
        devices, length = (lax.axis_size(axis), x.shape[dim])
        up = [(i, (i + 1) % devices) for i in range(devices - 1)]
        down = [(j, i) for i, j in up]
        last = lax.slice_in_dim(x, length - width, length, axis=dim)
        initial = lax.slice_in_dim(x, 0, width, axis=dim)
        before = lax.ppermute(last, axis, up)
        after = lax.ppermute(initial, axis, down)
        x = jnp.concatenate([before, x, after], axis=dim)
    return x


def passed_along(block, axis, distance):
    devices = range(lax.axis_size(axis))
    route = [(i - distance, i) for i in devices if i - distance in devices]
    return lax.ppermute(block, axis, route)


def along_cols(a):
    return 0.5 * (a[:, 1:-1, 2:] - a[:, 1:-1, :-2])


def along_rows(a):
    return 0.5 * (a[:, 2:, 1:-1] - a[:, :-2, 1:-1])


def laplace(a):
    return (
        a[:, 2:, 1:-1] + a[:, :-2, 1:-1] + a[:, 1:-1, 2:] + a[:, 1:-1, :-2] - 4.0 * a[:, 1:-1, 1:-1]
    )


def advance(padded, drag, coriolis):
    levels = padded[:, 1:-1]
    thick, zonal, merid = (levels[0], levels[1], levels[2])
    centre = padded[:, 1:-1, 1:-1, 1:-1]
    h_c, u_c, v_c = (centre[0], centre[1], centre[2])
    rot = coriolis[None, :, None]
    rate = drag[:, None, None]
    vert = padded[:, 2:, 1:-1, 1:-1] + padded[:, :-2, 1:-1, 1:-1] - 2.0 * centre
    u_new = (
        u_c
        + time_step
        * (
            -along_cols(thick)
            - u_c * along_cols(zonal)
            - v_c * along_rows(zonal)
            + rot * v_c
            - rate * u_c
        )
        + viscosity * laplace(zonal)
    )
    v_new = (
        v_c
        + time_step
        * (
            -along_rows(thick)
            - u_c * along_cols(merid)
            - v_c * along_rows(merid)
            - rot * u_c
            - rate * v_c
        )
        + viscosity * laplace(merid)
    )
    h_new = (
        h_c
        - time_step
        * (
            along_cols(zonal)
            + along_rows(merid)
            + along_cols(thick * zonal)
            + along_rows(thick * merid)
        )
        + viscosity * laplace(thick)
    )
    return jnp.stack([h_new, u_new, v_new]) + vertical_mix * vert


def extend(state):
    return with_halo(state, (("gx", 2), ("col", 3), ("gz", 1)), 1)


def halo_back(cot):
    inner = cot[:, 1:-1, 1:-1, 1:-1]
    below = passed_along(cot[:, 0, 1:-1, 1:-1], "gz", -1)
    above = passed_along(cot[:, -1, 1:-1, 1:-1], "gz", 1)
    inner = inner.at[:, -1].add(below).at[:, 0].add(above)
    south = passed_along(cot[:, 1:-1, 0, 1:-1], "gx", -1)
    north = passed_along(cot[:, 1:-1, -1, 1:-1], "gx", 1)
    inner = inner.at[:, :, -1].add(south).at[:, :, 0].add(north)
    west = passed_along(cot[:, 1:-1, 1:-1, 0], "col", -1)
    east = passed_along(cot[:, 1:-1, 1:-1, -1], "col", 1)
    return inner.at[:, :, :, -1].add(west).at[:, :, :, 0].add(east)


def on_device(checkpoints, obs_values, obs_mask, drag):
    lat_count = obs_values.shape[2]
    lon_count = obs_values.shape[3]
    segments = obs_values.shape[0]
    total_lat = lat_count * lax.axis_size("gx")
    total_lon = lon_count * lax.axis_size("col")
    rows = (lax.axis_index("gx") * lat_count + jnp.arange(lat_count)).astype(jnp.float32)
    cols = (lax.axis_index("col") * lon_count + jnp.arange(lon_count)).astype(jnp.float32)
    coriolis = 0.2 + 0.1 * rows / total_lat
    weight = (1.0 + 2.0 * rows / total_lat)[:, None] * (1.0 + 2.0 * cols / total_lon)[None, :]
    owned_cols = lax.all_to_all(checkpoints, "col", split_axis=4, concat_axis=0, tiled=True)

    def local(padded, rate):
        return advance(padded, rate, coriolis)

    levels = drag.shape[0]
    adjoint = jnp.zeros((3, levels, lat_count, lon_count), jnp.float32)
    cost = jnp.zeros((levels,), jnp.float32)
    drag_total = jnp.zeros((levels,), jnp.float32)
    for seg in reversed(range(segments)):
        state = owned_cols[seg].astype(jnp.float32)
        pads = []
        for step in range(SEG):
            padded = extend(state)
            pads.append(padded)
            state = advance(padded, drag, coriolis)
        resid = state[0] - obs_values[seg]
        forcing = weight[None] * obs_mask[seg].astype(jnp.float32) * resid
        seg_cost = 0.5 * jnp.sum(forcing * resid, axis=(1, 2))
        adjoint = adjoint.at[0].add(forcing)
        seg_drag = jnp.zeros((levels,), jnp.float32)
        for step in reversed(range(SEG)):
            unused, pull = jax.vjp(local, pads[step], drag)
            cot_pad, cot_drag = pull(adjoint)
            seg_drag = seg_drag + cot_drag
            adjoint = halo_back(cot_pad)
        summed_drag, summed_cost = lax.psum((seg_drag, seg_cost), ("gx", "col"))
        drag_total = drag_total + summed_drag
        cost = cost + summed_cost
    scale = 1.0 / (total_lat * total_lon)
    return (adjoint, cost * scale, drag_total * scale)


def solution(mesh):
    return jax.shard_map(
        on_device,
        mesh=mesh,
        in_specs=(
            P(("ens", "col"), None, "gz", "gx", None),
            P("ens", "gz", "gx", "col"),
            P("ens", "gz", "gx", "col"),
            P(("ens", "gz")),
        ),
        out_specs=(P("ens", "gz", "gx", "col"), P(("ens", "gz")), P(("ens", "gz"))),
        check_vma=False,
    )
```

profile of v0, /device:TPU:0, one launch (start us, length us, event | category | flops | bytes accessed | tf_op | source)
XLA Modules:
  0.0 335.3 jit_solution(2285676061232083874)
XLA Ops:
  4.5 4.4 %all-to-all-start = ((bf16[2,2,12288]{2,1,0:T(2,128)(2,1)}), bf16[2,2,12288]{2,1,0:T(2,128)(2,1)S(1)}, u32[]{:S(2)}, u32[]{:S(2)}) async-start(bf16[2,2,12288]{2,1,0:T(2,128)(2,1)} %reshape.2001), calls=%async_computation | async-start | bytes 196608 | tf_op jit(solution)/shard_map/all_to_all | solution.py:118
  10.6 2.6 all-to-all-done
  14.7 4.0 %collective-permute-start = (f32[3,16,1,128]{3,1,2,0:T(8,128)S(1)}, f32[3,16,1,128]{3,1,2,0:T(8,128)S(1)}, u32[]{:S(2)}, u32[]{:S(2)}) collective-permute-start(f32[3,16,1,128]{3,1,2,0:T(8,128)S(1)} %get-tuple-element.1053), channel_id=1, source_target_pairs={{0,4},{4,8},{8,12},{1,5},{5,9},{9,13},{2,6},{6,10},{10,14},{3,7},{... | collective-permute-start | bytes 73736 | tf_op jit(solution)/shard_map/ppermute | solution.py:19
  20.0 4.5 %collective-permute-start.24 = (f32[3,16,1,128]{3,1,2,0:T(8,128)S(1)}, f32[3,16,1,128]{3,1,2,0:T(8,128)S(1)}, u32[]{:S(2)}, u32[]{:S(2)}) collective-permute-start(f32[3,16,1,128]{3,1,2,0:T(8,128)S(1)} %get-tuple-element.1057), channel_id=1, source_target_pairs={{0,4},{4,8},{8,12},{1,5},{5,9},{9,13},{2,6},{6,10},{10,14},{3,7},{... | collective-permute-start | bytes 73736 | tf_op jit(solution)/shard_map/ppermute | solution.py:19
  25.9 4.5 %collective-permute-start.48 = (f32[3,16,1,128]{3,1,2,0:T(8,128)S(1)}, f32[3,16,1,128]{3,1,2,0:T(8,128)S(1)}, u32[]{:S(2)}, u32[]{:S(2)}) collective-permute-start(f32[3,16,1,128]{3,1,2,0:T(8,128)S(1)} %get-tuple-element.1061), channel_id=1, source_target_pairs={{0,4},{4,8},{8,12},{1,5},{5,9},{9,13},{2,6},{6,10},{10,14},{3,7},{... | collective-permute-start | bytes 73736 | tf_op jit(solution)/shard_map/ppermute | solution.py:19
  31.8 4.5 %collective-permute-start.72 = (f32[3,16,1,128]{3,1,2,0:T(8,128)S(1)}, f32[3,16,1,128]{3,1,2,0:T(8,128)S(1)}, u32[]{:S(2)}, u32[]{:S(2)}) collective-permute-start(f32[3,16,1,128]{3,1,2,0:T(8,128)S(1)} %get-tuple-element.1065), channel_id=1, source_target_pairs={{0,4},{4,8},{8,12},{1,5},{5,9},{9,13},{2,6},{6,10},{10,14},{3,7},{... | collective-permute-start | bytes 73736 | tf_op jit(solution)/shard_map/ppermute | solution.py:19
  41.1 4.6 %collective-permute-start.26 = (f32[3,16,4,1]{3,1,2,0:T(8,128)S(1)}, f32[3,16,4,1]{3,1,2,0:T(8,128)S(1)}, u32[]{:S(2)}, u32[]{:S(2)}) collective-permute-start(f32[3,16,4,1]{3,1,2,0:T(8,128)S(1)} %get-tuple-element.948), channel_id=1, source_target_pairs={{0,2},{1,3},{4,6},{5,7},{8,10},{9,11},{12,14},{13,15},{16,18},{17,... | collective-permute-start | bytes 2312 | tf_op jit(solution)/shard_map/ppermute | solution.py:19
  47.1 4.6 %collective-permute-start.50 = (f32[3,16,4,1]{3,1,2,0:T(8,128)S(1)}, f32[3,16,4,1]{3,1,2,0:T(8,128)S(1)}, u32[]{:S(2)}, u32[]{:S(2)}) collective-permute-start(f32[3,16,4,1]{3,1,2,0:T(8,128)S(1)} %get-tuple-element.952), channel_id=1, source_target_pairs={{0,2},{1,3},{4,6},{5,7},{8,10},{9,11},{12,14},{13,15},{16,18},{17,... | collective-permute-start | bytes 2312 | tf_op jit(solution)/shard_map/ppermute | solution.py:19
  53.1 4.6 %collective-permute-start.74 = (f32[3,16,4,1]{3,1,2,0:T(8,128)S(1)}, f32[3,16,4,1]{3,1,2,0:T(8,128)S(1)}, u32[]{:S(2)}, u32[]{:S(2)}) collective-permute-start(f32[3,16,4,1]{3,1,2,0:T(8,128)S(1)} %get-tuple-element.956), channel_id=1, source_target_pairs={{0,2},{1,3},{4,6},{5,7},{8,10},{9,11},{12,14},{13,15},{16,18},{17,... | collective-permute-start | bytes 2312 | tf_op jit(solution)/shard_map/ppermute | solution.py:19
  59.8 4.5 %collective-permute-done.75 = f32[3,16,4,1]{3,1,2,0:T(8,128)S(1)} collective-permute-done((f32[3,16,4,1]{3,1,2,0:T(8,128)S(1)}, f32[3,16,4,1]{3,1,2,0:T(8,128)S(1)}, u32[]{:S(2)}, u32[]{:S(2)}) %collective-permute-start.75) | collective-permute-done | bytes 800 | tf_op jit(solution)/shard_map/ppermute | solution.py:20
  66.2 3.0 collective-permute-start.5
  70.9 3.0 collective-permute-start.29
  76.5 3.0 collective-permute-start.53
  81.0 3.0 collective-permute-start.77
  84.0 4.5 %collective-permute-start.6 = (f32[3,16,1,128]{3,1,2,0:T(8,128)S(1)}, f32[3,16,1,128]{3,1,2,0:T(8,128)S(1)}, u32[]{:S(2)}, u32[]{:S(2)}) collective-permute-start(f32[3,16,1,128]{3,1,2,0:T(8,128)S(1)} %get-tuple-element.1051), channel_id=1, source_target_pairs={{0,4},{4,8},{8,12},{1,5},{5,9},{9,13},{2,6},{6,10},{10,14},{3,7},{... | collective-permute-start | bytes 73736 | tf_op jit(solution)/shard_map/ppermute | solution.py:19
  90.0 4.5 %collective-permute-start.30 = (f32[3,16,1,128]{3,1,2,0:T(8,128)S(1)}, f32[3,16,1,128]{3,1,2,0:T(8,128)S(1)}, u32[]{:S(2)}, u32[]{:S(2)}) collective-permute-start(f32[3,16,1,128]{3,1,2,0:T(8,128)S(1)} %get-tuple-element.1055), channel_id=1, source_target_pairs={{0,4},{4,8},{8,12},{1,5},{5,9},{9,13},{2,6},{6,10},{10,14},{3,7},{... | collective-permute-start | bytes 73736 | tf_op jit(solution)/shard_map/ppermute | solution.py:19
  96.0 4.5 %collective-permute-start.54 = (f32[3,16,1,128]{3,1,2,0:T(8,128)S(1)}, f32[3,16,1,128]{3,1,2,0:T(8,128)S(1)}, u32[]{:S(2)}, u32[]{:S(2)}) collective-permute-start(f32[3,16,1,128]{3,1,2,0:T(8,128)S(1)} %get-tuple-element.1059), channel_id=1, source_target_pairs={{0,4},{4,8},{8,12},{1,5},{5,9},{9,13},{2,6},{6,10},{10,14},{3,7},{... | collective-permute-start | bytes 73736 | tf_op jit(solution)/shard_map/ppermute | solution.py:19
  102.0 4.5 %collective-permute-start.78 = (f32[3,16,1,128]{3,1,2,0:T(8,128)S(1)}, f32[3,16,1,128]{3,1,2,0:T(8,128)S(1)}, u32[]{:S(2)}, u32[]{:S(2)}) collective-permute-start(f32[3,16,1,128]{3,1,2,0:T(8,128)S(1)} %get-tuple-element.1063), channel_id=1, source_target_pairs={{0,4},{4,8},{8,12},{1,5},{5,9},{9,13},{2,6},{6,10},{10,14},{3,7},{... | collective-permute-start | bytes 73736 | tf_op jit(solution)/shard_map/ppermute | solution.py:19
  111.0 4.6 %collective-permute-start.32 = (f32[3,16,4,1]{3,1,2,0:T(8,128)S(1)}, f32[3,16,4,1]{3,1,2,0:T(8,128)S(1)}, u32[]{:S(2)}, u32[]{:S(2)}) collective-permute-start(f32[3,16,4,1]{3,1,2,0:T(8,128)S(1)} %get-tuple-element.946), channel_id=1, source_target_pairs={{0,2},{1,3},{4,6},{5,7},{8,10},{9,11},{12,14},{13,15},{16,18},{17,... | collective-permute-start | bytes 2312 | tf_op jit(solution)/shard_map/ppermute | solution.py:19
  117.0 4.6 %collective-permute-start.56 = (f32[3,16,4,1]{3,1,2,0:T(8,128)S(1)}, f32[3,16,4,1]{3,1,2,0:T(8,128)S(1)}, u32[]{:S(2)}, u32[]{:S(2)}) collective-permute-start(f32[3,16,4,1]{3,1,2,0:T(8,128)S(1)} %get-tuple-element.950), channel_id=1, source_target_pairs={{0,2},{1,3},{4,6},{5,7},{8,10},{9,11},{12,14},{13,15},{16,18},{17,... | collective-permute-start | bytes 2312 | tf_op jit(solution)/shard_map/ppermute | solution.py:19
  123.0 4.6 %collective-permute-start.80 = (f32[3,16,4,1]{3,1,2,0:T(8,128)S(1)}, f32[3,16,4,1]{3,1,2,0:T(8,128)S(1)}, u32[]{:S(2)}, u32[]{:S(2)}) collective-permute-start(f32[3,16,4,1]{3,1,2,0:T(8,128)S(1)} %get-tuple-element.954), channel_id=1, source_target_pairs={{0,2},{1,3},{4,6},{5,7},{8,10},{9,11},{12,14},{13,15},{16,18},{17,... | collective-permute-start | bytes 2312 | tf_op jit(solution)/shard_map/ppermute | solution.py:19
  129.7 4.5 %collective-permute-done.81 = f32[3,16,4,1]{3,1,2,0:T(8,128)S(1)} collective-permute-done((f32[3,16,4,1]{3,1,2,0:T(8,128)S(1)}, f32[3,16,4,1]{3,1,2,0:T(8,128)S(1)}, u32[]{:S(2)}, u32[]{:S(2)}) %collective-permute-start.81) | collective-permute-done | bytes 800 | tf_op jit(solution)/shard_map/ppermute | solution.py:20
  136.1 3.0 collective-permute-start.11
  140.8 3.0 collective-permute-start.35
  146.8 3.0 collective-permute-start.59
  151.2 3.0 collective-permute-start.83
  160.7 4.5 %collective-permute-start.17 = (f32[3,16,2]{1,2,0:T(2,128)S(1)}, f32[3,16,2]{1,2,0:T(2,128)S(1)}, u32[]{:S(2)}, u32[]{:S(2)}) collective-permute-start(f32[3,16,2]{1,2,0:T(2,128)S(1)} %get-tuple-element.662), channel_id=1, source_target_pairs={{0,2},{1,3},{4,6},{5,7},{8,10},{9,11},{12,14},{13,15},{16,18},{17,... | collective-permute-start | bytes 1160 | tf_op jit(solution)/shard_map/ppermute | solution.py:28
  165.5 2.7 collective-permute-start.13
  168.2 5.2 %collective-permute-start.15 = (f32[3,16,128]{2,1,0:T(8,128)S(1)}, f32[3,16,128]{2,1,0:T(8,128)S(1)}, u32[]{:S(2)}, u32[]{:S(2)}) collective-permute-start(f32[3,16,128]{2,1,0:T(8,128)S(1)} %get-tuple-element.794), channel_id=1, source_target_pairs={{0,4},{4,8},{8,12},{1,5},{5,9},{9,13},{2,6},{6,10},{10,14},{3,7},{... | collective-permute-start | bytes 73736 | tf_op jit(solution)/shard_map/ppermute | solution.py:28
  181.1 4.5 %collective-permute-start.23 = (f32[3,16,2]{1,2,0:T(2,128)S(1)}, f32[3,16,2]{1,2,0:T(2,128)S(1)}, u32[]{:S(2)}, u32[]{:S(2)}) collective-permute-start(f32[3,16,2]{1,2,0:T(2,128)S(1)} %get-tuple-element.660), channel_id=1, source_target_pairs={{0,2},{1,3},{4,6},{5,7},{8,10},{9,11},{12,14},{13,15},{16,18},{17,... | collective-permute-start | bytes 1160 | tf_op jit(solution)/shard_map/ppermute | solution.py:28
  185.7 2.5 collective-permute-start.19
  188.2 4.8 %collective-permute-start.21 = (f32[3,16,128]{2,1,0:T(8,128)S(1)}, f32[3,16,128]{2,1,0:T(8,128)S(1)}, u32[]{:S(2)}, u32[]{:S(2)}) collective-permute-start(f32[3,16,128]{2,1,0:T(8,128)S(1)} %get-tuple-element.789), channel_id=1, source_target_pairs={{0,4},{4,8},{8,12},{1,5},{5,9},{9,13},{2,6},{6,10},{10,14},{3,7},{... | collective-permute-start | bytes 73736 | tf_op jit(solution)/shard_map/ppermute | solution.py:28
  199.3 3.0 collective-permute-start.37
  202.4 4.3 %collective-permute-start.41 = (f32[3,16,2]{1,2,0:T(2,128)S(1)}, f32[3,16,2]{1,2,0:T(2,128)S(1)}, u32[]{:S(2)}, u32[]{:S(2)}) collective-permute-start(f32[3,16,2]{1,2,0:T(2,128)S(1)} %bitcast.1257), channel_id=1, source_target_pairs={{0,2},{1,3},{4,6},{5,7},{8,10},{9,11},{12,14},{13,15},{16,18},{17,... | collective-permute-start | bytes 1160 | tf_op jit(solution)/shard_map/ppermute | solution.py:28
  208.0 4.8 %collective-permute-start.39 = (f32[3,16,128]{2,1,0:T(8,128)S(1)}, f32[3,16,128]{2,1,0:T(8,128)S(1)}, u32[]{:S(2)}, u32[]{:S(2)}) collective-permute-start(f32[3,16,128]{2,1,0:T(8,128)S(1)} %get-tuple-element.785), channel_id=1, source_target_pairs={{0,4},{4,8},{8,12},{1,5},{5,9},{9,13},{2,6},{6,10},{10,14},{3,7},{... | collective-permute-start | bytes 73736 | tf_op jit(solution)/shard_map/ppermute | solution.py:28
  220.4 4.5 %collective-permute-start.47 = (f32[3,16,2]{1,2,0:T(2,128)S(1)}, f32[3,16,2]{1,2,0:T(2,128)S(1)}, u32[]{:S(2)}, u32[]{:S(2)}) collective-permute-start(f32[3,16,2]{1,2,0:T(2,128)S(1)} %get-tuple-element.658), channel_id=1, source_target_pairs={{0,2},{1,3},{4,6},{5,7},{8,10},{9,11},{12,14},{13,15},{16,18},{17,... | collective-permute-start | bytes 1160 | tf_op jit(solution)/shard_map/ppermute | solution.py:28
  227.5 4.8 %collective-permute-start.45 = (f32[3,16,128]{2,1,0:T(8,128)S(1)}, f32[3,16,128]{2,1,0:T(8,128)S(1)}, u32[]{:S(2)}, u32[]{:S(2)}) collective-permute-start(f32[3,16,128]{2,1,0:T(8,128)S(1)} %get-tuple-element.778), channel_id=1, source_target_pairs={{0,4},{4,8},{8,12},{1,5},{5,9},{9,13},{2,6},{6,10},{10,14},{3,7},{... | collective-permute-start | bytes 73736 | tf_op jit(solution)/shard_map/ppermute | solution.py:28
  238.6 3.0 collective-permute-start.61
  241.7 4.3 %collective-permute-start.65 = (f32[3,16,2]{1,2,0:T(2,128)S(1)}, f32[3,16,2]{1,2,0:T(2,128)S(1)}, u32[]{:S(2)}, u32[]{:S(2)}) collective-permute-start(f32[3,16,2]{1,2,0:T(2,128)S(1)} %bitcast.1261), channel_id=1, source_target_pairs={{0,2},{1,3},{4,6},{5,7},{8,10},{9,11},{12,14},{13,15},{16,18},{17,... | collective-permute-start | bytes 1160 | tf_op jit(solution)/shard_map/ppermute | solution.py:28
  247.3 4.8 %collective-permute-start.63 = (f32[3,16,128]{2,1,0:T(8,128)S(1)}, f32[3,16,128]{2,1,0:T(8,128)S(1)}, u32[]{:S(2)}, u32[]{:S(2)}) collective-permute-start(f32[3,16,128]{2,1,0:T(8,128)S(1)} %get-tuple-element.774), channel_id=1, source_target_pairs={{0,4},{4,8},{8,12},{1,5},{5,9},{9,13},{2,6},{6,10},{10,14},{3,7},{... | collective-permute-start | bytes 73736 | tf_op jit(solution)/shard_map/ppermute | solution.py:28
  259.7 4.5 %collective-permute-start.71 = (f32[3,16,2]{1,2,0:T(2,128)S(1)}, f32[3,16,2]{1,2,0:T(2,128)S(1)}, u32[]{:S(2)}, u32[]{:S(2)}) collective-permute-start(f32[3,16,2]{1,2,0:T(2,128)S(1)} %get-tuple-element.656), channel_id=1, source_target_pairs={{0,2},{1,3},{4,6},{5,7},{8,10},{9,11},{12,14},{13,15},{16,18},{17,... | collective-permute-start | bytes 1160 | tf_op jit(solution)/shard_map/ppermute | solution.py:28
  266.7 4.8 %collective-permute-start.69 = (f32[3,16,128]{2,1,0:T(8,128)S(1)}, f32[3,16,128]{2,1,0:T(8,128)S(1)}, u32[]{:S(2)}, u32[]{:S(2)}) collective-permute-start(f32[3,16,128]{2,1,0:T(8,128)S(1)} %get-tuple-element.767), channel_id=1, source_target_pairs={{0,4},{4,8},{8,12},{1,5},{5,9},{9,13},{2,6},{6,10},{10,14},{3,7},{... | collective-permute-start | bytes 73736 | tf_op jit(solution)/shard_map/ppermute | solution.py:28
  277.9 3.0 collective-permute-start.85
  281.0 4.3 %collective-permute-start.89 = (f32[3,16,2]{1,2,0:T(2,128)S(1)}, f32[3,16,2]{1,2,0:T(2,128)S(1)}, u32[]{:S(2)}, u32[]{:S(2)}) collective-permute-start(f32[3,16,2]{1,2,0:T(2,128)S(1)} %bitcast.1265), channel_id=1, source_target_pairs={{0,2},{1,3},{4,6},{5,7},{8,10},{9,11},{12,14},{13,15},{16,18},{17,... | collective-permute-start | bytes 1160 | tf_op jit(solution)/shard_map/ppermute | solution.py:28
  286.6 4.8 %collective-permute-start.87 = (f32[3,16,128]{2,1,0:T(8,128)S(1)}, f32[3,16,128]{2,1,0:T(8,128)S(1)}, u32[]{:S(2)}, u32[]{:S(2)}) collective-permute-start(f32[3,16,128]{2,1,0:T(8,128)S(1)} %get-tuple-element.763), channel_id=1, source_target_pairs={{0,4},{4,8},{8,12},{1,5},{5,9},{9,13},{2,6},{6,10},{10,14},{3,7},{... | collective-permute-start | bytes 73736 | tf_op jit(solution)/shard_map/ppermute | solution.py:28
  294.8 21.1 %all-reduce.312 = (f32[16]{0:T(128)S(1)}, f32[16]{0:T(128)S(1)}) all-reduce(f32[16]{0:T(128)S(1)} %add_multiply_fusion, f32[16]{0:T(128)S(1)} %add_add_fusion.1), channel_id=1, replica_groups=mesh['ens'=2,'gx'=4,'col'=2,'gz'=2] {'gx','col'}, use_global_device_ids=true, to_apply=%region_1.0 | all-reduce | flops 32 | bytes 256 | tf_op jit(solution)/shard_map/psum | solution.py:144
  321.2 4.5 %collective-permute-start.95 = (f32[3,16,2]{1,2,0:T(2,128)S(1)}, f32[3,16,2]{1,2,0:T(2,128)S(1)}, u32[]{:S(2)}, u32[]{:S(2)}) collective-permute-start(f32[3,16,2]{1,2,0:T(2,128)S(1)} %get-tuple-element.654), channel_id=1, source_target_pairs={{0,2},{1,3},{4,6},{5,7},{8,10},{9,11},{12,14},{13,15},{16,18},{17,... | collective-permute-start | bytes 1160 | tf_op jit(solution)/shard_map/ppermute | solution.py:28
  328.2 4.3 %collective-permute-start.93 = (f32[3,16,128]{2,1,0:T(8,128)S(1)}, f32[3,16,128]{2,1,0:T(8,128)S(1)}, u32[]{:S(2)}, u32[]{:S(2)}) collective-permute-start(f32[3,16,128]{2,1,0:T(8,128)S(1)} %get-tuple-element.756), channel_id=1, source_target_pairs={{0,4},{4,8},{8,12},{1,5},{5,9},{9,13},{2,6},{6,10},{10,14},{3,7},{... | collective-permute-start | bytes 73736 | tf_op jit(solution)/shard_map/ppermute | solution.py:28
  (500 shorter events, 118.9 us)
Async XLA Ops:
  14.7 15.8 %collective-permute-start = (f32[3,16,1,128]{3,1,2,0:T(8,128)S(1)}, f32[3,16,1,128]{3,1,2,0:T(8,128)S(1)}, u32[]{:S(2)}, u32[]{:S(2)}) collective-permute-start(f32[3,16,1,128]{3,1,2,0:T(8,128)S(1)} %get-tuple-element.1053), channel_id=1, source_target_pairs={{0,4},{4,8},{8,12},{1,5},{5,9},{9,13},{2,6},{6,10},{10,14},{3,7},{... | collective-permute-start | bytes 73736 | tf_op jit(solution)/shard_map/ppermute | solution.py:19
  18.7 13.1 %collective-permute-start.1 = (f32[3,16,1,128]{3,1,2,0:T(8,128)S(1)}, f32[3,16,1,128]{3,1,2,0:T(8,128)S(1)}, u32[]{:S(2)}, u32[]{:S(2)}) collective-permute-start(f32[3,16,1,128]{3,1,2,0:T(8,128)S(1)} %get-tuple-element.1054), channel_id=1, source_target_pairs={{4,0},{8,4},{12,8},{5,1},{9,5},{13,9},{6,2},{10,6},{14,10},{7,3},{... | collective-permute-start | bytes 73736 | tf_op jit(solution)/shard_map/ppermute | solution.py:20
  20.0 16.4 %collective-permute-start.24 = (f32[3,16,1,128]{3,1,2,0:T(8,128)S(1)}, f32[3,16,1,128]{3,1,2,0:T(8,128)S(1)}, u32[]{:S(2)}, u32[]{:S(2)}) collective-permute-start(f32[3,16,1,128]{3,1,2,0:T(8,128)S(1)} %get-tuple-element.1057), channel_id=1, source_target_pairs={{0,4},{4,8},{8,12},{1,5},{5,9},{9,13},{2,6},{6,10},{10,14},{3,7},{... | collective-permute-start | bytes 73736 | tf_op jit(solution)/shard_map/ppermute | solution.py:19
  24.6 13.2 %collective-permute-start.25 = (f32[3,16,1,128]{3,1,2,0:T(8,128)S(1)}, f32[3,16,1,128]{3,1,2,0:T(8,128)S(1)}, u32[]{:S(2)}, u32[]{:S(2)}) collective-permute-start(f32[3,16,1,128]{3,1,2,0:T(8,128)S(1)} %get-tuple-element.1058), channel_id=1, source_target_pairs={{4,0},{8,4},{12,8},{5,1},{9,5},{13,9},{6,2},{10,6},{14,10},{7,3},{... | collective-permute-start | bytes 73736 | tf_op jit(solution)/shard_map/ppermute | solution.py:20
  25.9 13.9 %collective-permute-start.48 = (f32[3,16,1,128]{3,1,2,0:T(8,128)S(1)}, f32[3,16,1,128]{3,1,2,0:T(8,128)S(1)}, u32[]{:S(2)}, u32[]{:S(2)}) collective-permute-start(f32[3,16,1,128]{3,1,2,0:T(8,128)S(1)} %get-tuple-element.1061), channel_id=1, source_target_pairs={{0,4},{4,8},{8,12},{1,5},{5,9},{9,13},{2,6},{6,10},{10,14},{3,7},{... | collective-permute-start | bytes 73736 | tf_op jit(solution)/shard_map/ppermute | solution.py:19
  31.8 14.0 %collective-permute-start.72 = (f32[3,16,1,128]{3,1,2,0:T(8,128)S(1)}, f32[3,16,1,128]{3,1,2,0:T(8,128)S(1)}, u32[]{:S(2)}, u32[]{:S(2)}) collective-permute-start(f32[3,16,1,128]{3,1,2,0:T(8,128)S(1)} %get-tuple-element.1065), channel_id=1, source_target_pairs={{0,4},{4,8},{8,12},{1,5},{5,9},{9,13},{2,6},{6,10},{10,14},{3,7},{... | collective-permute-start | bytes 73736 | tf_op jit(solution)/shard_map/ppermute | solution.py:19
  37.8 14.0 %collective-permute-start.2 = (f32[3,16,4,1]{3,1,2,0:T(8,128)S(1)}, f32[3,16,4,1]{3,1,2,0:T(8,128)S(1)}, u32[]{:S(2)}, u32[]{:S(2)}) collective-permute-start(f32[3,16,4,1]{3,1,2,0:T(8,128)S(1)} %get-tuple-element.944), channel_id=1, source_target_pairs={{0,2},{1,3},{4,6},{5,7},{8,10},{9,11},{12,14},{13,15},{16,18},{17,... | collective-permute-start | bytes 2312 | tf_op jit(solution)/shard_map/ppermute | solution.py:19
  39.8 13.3 %collective-permute-start.3 = (f32[3,16,4,1]{3,1,2,0:T(8,128)S(1)}, f32[3,16,4,1]{3,1,2,0:T(8,128)S(1)}, u32[]{:S(2)}, u32[]{:S(2)}) collective-permute-start(f32[3,16,4,1]{3,1,2,0:T(8,128)S(1)} %get-tuple-element.945), channel_id=1, source_target_pairs={{2,0},{3,1},{6,4},{7,5},{10,8},{11,9},{14,12},{15,13},{18,16},{19,... | collective-permute-start | bytes 2312 | tf_op jit(solution)/shard_map/ppermute | solution.py:20
  41.1 16.7 %collective-permute-start.26 = (f32[3,16,4,1]{3,1,2,0:T(8,128)S(1)}, f32[3,16,4,1]{3,1,2,0:T(8,128)S(1)}, u32[]{:S(2)}, u32[]{:S(2)}) collective-permute-start(f32[3,16,4,1]{3,1,2,0:T(8,128)S(1)} %get-tuple-element.948), channel_id=1, source_target_pairs={{0,2},{1,3},{4,6},{5,7},{8,10},{9,11},{12,14},{13,15},{16,18},{17,... | collective-permute-start | bytes 2312 | tf_op jit(solution)/shard_map/ppermute | solution.py:19
  45.8 13.4 %collective-permute-start.27 = (f32[3,16,4,1]{3,1,2,0:T(8,128)S(1)}, f32[3,16,4,1]{3,1,2,0:T(8,128)S(1)}, u32[]{:S(2)}, u32[]{:S(2)}) collective-permute-start(f32[3,16,4,1]{3,1,2,0:T(8,128)S(1)} %get-tuple-element.949), channel_id=1, source_target_pairs={{2,0},{3,1},{6,4},{7,5},{10,8},{11,9},{14,12},{15,13},{18,16},{19,... | collective-permute-start | bytes 2312 | tf_op jit(solution)/shard_map/ppermute | solution.py:20
  47.1 12.3 %collective-permute-start.50 = (f32[3,16,4,1]{3,1,2,0:T(8,128)S(1)}, f32[3,16,4,1]{3,1,2,0:T(8,128)S(1)}, u32[]{:S(2)}, u32[]{:S(2)}) collective-permute-start(f32[3,16,4,1]{3,1,2,0:T(8,128)S(1)} %get-tuple-element.952), channel_id=1, source_target_pairs={{0,2},{1,3},{4,6},{5,7},{8,10},{9,11},{12,14},{13,15},{16,18},{17,... | collective-permute-start | bytes 2312 | tf_op jit(solution)/shard_map/ppermute | solution.py:19
  66.2 13.3 %collective-permute-start.5 = (f32[3,1,4,130]{3,1,2,0:T(1,128)S(1)}, f32[3,1,4,130]{3,1,2,0:T(1,128)S(1)}, u32[]{:S(2)}, u32[]{:S(2)}) collective-permute-start(f32[3,1,4,130]{3,1,2,0:T(1,128)S(1)} %get-tuple-element.801), channel_id=1, source_target_pairs={{0,1},{2,3},{4,5},{6,7},{8,9},{10,11},{12,13},{14,15},{16,17},{18,... | collective-permute-start | bytes 18728 | tf_op jit(solution)/shard_map/ppermute | solution.py:19
  70.9 13.1 %collective-permute-start.29 = (f32[3,1,4,130]{3,1,2,0:T(1,128)S(1)}, f32[3,1,4,130]{3,1,2,0:T(1,128)S(1)}, u32[]{:S(2)}, u32[]{:S(2)}) collective-permute-start(f32[3,1,4,130]{3,1,2,0:T(1,128)S(1)} %get-tuple-element.805), channel_id=1, source_target_pairs={{0,1},{2,3},{4,5},{6,7},{8,9},{10,11},{12,13},{14,15},{16,17},{18,... | collective-permute-start | bytes 18728 | tf_op jit(solution)/shard_map/ppermute | solution.py:19
  74.3 14.4 %collective-permute-start.52 = (f32[3,1,4,130]{3,1,2,0:T(1,128)S(1)}, f32[3,1,4,130]{3,1,2,0:T(1,128)S(1)}, u32[]{:S(2)}, u32[]{:S(2)}) collective-permute-start(f32[3,1,4,130]{3,1,2,0:T(1,128)S(1)} %get-tuple-element.808), channel_id=1, source_target_pairs={{1,0},{3,2},{5,4},{7,6},{9,8},{11,10},{13,12},{15,14},{17,16},{19,... | collective-permute-start | bytes 18728 | tf_op jit(solution)/shard_map/ppermute | solution.py:20
  76.5 13.5 %collective-permute-start.53 = (f32[3,1,4,130]{3,1,2,0:T(1,128)S(1)}, f32[3,1,4,130]{3,1,2,0:T(1,128)S(1)}, u32[]{:S(2)}, u32[]{:S(2)}) collective-permute-start(f32[3,1,4,130]{3,1,2,0:T(1,128)S(1)} %get-tuple-element.809), channel_id=1, source_target_pairs={{0,1},{2,3},{4,5},{6,7},{8,9},{10,11},{12,13},{14,15},{16,17},{18,... | collective-permute-start | bytes 18728 | tf_op jit(solution)/shard_map/ppermute | solution.py:19
  79.5 15.2 %collective-permute-start.76 = (f32[3,1,4,130]{3,1,2,0:T(1,128)S(1)}, f32[3,1,4,130]{3,1,2,0:T(1,128)S(1)}, u32[]{:S(2)}, u32[]{:S(2)}) collective-permute-start(f32[3,1,4,130]{3,1,2,0:T(1,128)S(1)} %get-tuple-element.812), channel_id=1, source_target_pairs={{1,0},{3,2},{5,4},{7,6},{9,8},{11,10},{13,12},{15,14},{17,16},{19,... | collective-permute-start | bytes 18728 | tf_op jit(solution)/shard_map/ppermute | solution.py:20
  81.0 15.1 %collective-permute-start.77 = (f32[3,1,4,130]{3,1,2,0:T(1,128)S(1)}, f32[3,1,4,130]{3,1,2,0:T(1,128)S(1)}, u32[]{:S(2)}, u32[]{:S(2)}) collective-permute-start(f32[3,1,4,130]{3,1,2,0:T(1,128)S(1)} %get-tuple-element.813), channel_id=1, source_target_pairs={{0,1},{2,3},{4,5},{6,7},{8,9},{10,11},{12,13},{14,15},{16,17},{18,... | collective-permute-start | bytes 18728 | tf_op jit(solution)/shard_map/ppermute | solution.py:19
  84.0 16.7 %collective-permute-start.6 = (f32[3,16,1,128]{3,1,2,0:T(8,128)S(1)}, f32[3,16,1,128]{3,1,2,0:T(8,128)S(1)}, u32[]{:S(2)}, u32[]{:S(2)}) collective-permute-start(f32[3,16,1,128]{3,1,2,0:T(8,128)S(1)} %get-tuple-element.1051), channel_id=1, source_target_pairs={{0,4},{4,8},{8,12},{1,5},{5,9},{9,13},{2,6},{6,10},{10,14},{3,7},{... | collective-permute-start | bytes 73736 | tf_op jit(solution)/shard_map/ppermute | solution.py:19
  88.7 13.3 %collective-permute-start.7 = (f32[3,16,1,128]{3,1,2,0:T(8,128)S(1)}, f32[3,16,1,128]{3,1,2,0:T(8,128)S(1)}, u32[]{:S(2)}, u32[]{:S(2)}) collective-permute-start(f32[3,16,1,128]{3,1,2,0:T(8,128)S(1)} %get-tuple-element.1052), channel_id=1, source_target_pairs={{4,0},{8,4},{12,8},{5,1},{9,5},{13,9},{6,2},{10,6},{14,10},{7,3},{... | collective-permute-start | bytes 73736 | tf_op jit(solution)/shard_map/ppermute | solution.py:20
  90.0 16.7 %collective-permute-start.30 = (f32[3,16,1,128]{3,1,2,0:T(8,128)S(1)}, f32[3,16,1,128]{3,1,2,0:T(8,128)S(1)}, u32[]{:S(2)}, u32[]{:S(2)}) collective-permute-start(f32[3,16,1,128]{3,1,2,0:T(8,128)S(1)} %get-tuple-element.1055), channel_id=1, source_target_pairs={{0,4},{4,8},{8,12},{1,5},{5,9},{9,13},{2,6},{6,10},{10,14},{3,7},{... | collective-permute-start | bytes 73736 | tf_op jit(solution)/shard_map/ppermute | solution.py:19
  94.7 13.3 %collective-permute-start.31 = (f32[3,16,1,128]{3,1,2,0:T(8,128)S(1)}, f32[3,16,1,128]{3,1,2,0:T(8,128)S(1)}, u32[]{:S(2)}, u32[]{:S(2)}) collective-permute-start(f32[3,16,1,128]{3,1,2,0:T(8,128)S(1)} %get-tuple-element.1056), channel_id=1, source_target_pairs={{4,0},{8,4},{12,8},{5,1},{9,5},{13,9},{6,2},{10,6},{14,10},{7,3},{... | collective-permute-start | bytes 73736 | tf_op jit(solution)/shard_map/ppermute | solution.py:20
  96.0 13.6 %collective-permute-start.54 = (f32[3,16,1,128]{3,1,2,0:T(8,128)S(1)}, f32[3,16,1,128]{3,1,2,0:T(8,128)S(1)}, u32[]{:S(2)}, u32[]{:S(2)}) collective-permute-start(f32[3,16,1,128]{3,1,2,0:T(8,128)S(1)} %get-tuple-element.1059), channel_id=1, source_target_pairs={{0,4},{4,8},{8,12},{1,5},{5,9},{9,13},{2,6},{6,10},{10,14},{3,7},{... | collective-permute-start | bytes 73736 | tf_op jit(solution)/shard_map/ppermute | solution.py:19
  102.0 13.6 %collective-permute-start.78 = (f32[3,16,1,128]{3,1,2,0:T(8,128)S(1)}, f32[3,16,1,128]{3,1,2,0:T(8,128)S(1)}, u32[]{:S(2)}, u32[]{:S(2)}) collective-permute-start(f32[3,16,1,128]{3,1,2,0:T(8,128)S(1)} %get-tuple-element.1063), channel_id=1, source_target_pairs={{0,4},{4,8},{8,12},{1,5},{5,9},{9,13},{2,6},{6,10},{10,14},{3,7},{... | collective-permute-start | bytes 73736 | tf_op jit(solution)/shard_map/ppermute | solution.py:19
  108.0 13.6 %collective-permute-start.8 = (f32[3,16,4,1]{3,1,2,0:T(8,128)S(1)}, f32[3,16,4,1]{3,1,2,0:T(8,128)S(1)}, u32[]{:S(2)}, u32[]{:S(2)}) collective-permute-start(f32[3,16,4,1]{3,1,2,0:T(8,128)S(1)} %get-tuple-element.934), channel_id=1, source_target_pairs={{0,2},{1,3},{4,6},{5,7},{8,10},{9,11},{12,14},{13,15},{16,18},{17,... | collective-permute-start | bytes 2312 | tf_op jit(solution)/shard_map/ppermute | solution.py:19
  109.7 13.3 %collective-permute-start.9 = (f32[3,16,4,1]{3,1,2,0:T(8,128)S(1)}, f32[3,16,4,1]{3,1,2,0:T(8,128)S(1)}, u32[]{:S(2)}, u32[]{:S(2)}) collective-permute-start(f32[3,16,4,1]{3,1,2,0:T(8,128)S(1)} %get-tuple-element.935), channel_id=1, source_target_pairs={{2,0},{3,1},{6,4},{7,5},{10,8},{11,9},{14,12},{15,13},{18,16},{19,... | collective-permute-start | bytes 2312 | tf_op jit(solution)/shard_map/ppermute | solution.py:20
  111.0 16.7 %collective-permute-start.32 = (f32[3,16,4,1]{3,1,2,0:T(8,128)S(1)}, f32[3,16,4,1]{3,1,2,0:T(8,128)S(1)}, u32[]{:S(2)}, u32[]{:S(2)}) collective-permute-start(f32[3,16,4,1]{3,1,2,0:T(8,128)S(1)} %get-tuple-element.946), channel_id=1, source_target_pairs={{0,2},{1,3},{4,6},{5,7},{8,10},{9,11},{12,14},{13,15},{16,18},{17,... | collective-permute-start | bytes 2312 | tf_op jit(solution)/shard_map/ppermute | solution.py:19
  115.7 13.4 %collective-permute-start.33 = (f32[3,16,4,1]{3,1,2,0:T(8,128)S(1)}, f32[3,16,4,1]{3,1,2,0:T(8,128)S(1)}, u32[]{:S(2)}, u32[]{:S(2)}) collective-permute-start(f32[3,16,4,1]{3,1,2,0:T(8,128)S(1)} %get-tuple-element.947), channel_id=1, source_target_pairs={{2,0},{3,1},{6,4},{7,5},{10,8},{11,9},{14,12},{15,13},{18,16},{19,... | collective-permute-start | bytes 2312 | tf_op jit(solution)/shard_map/ppermute | solution.py:20
  117.0 12.3 %collective-permute-start.56 = (f32[3,16,4,1]{3,1,2,0:T(8,128)S(1)}, f32[3,16,4,1]{3,1,2,0:T(8,128)S(1)}, u32[]{:S(2)}, u32[]{:S(2)}) collective-permute-start(f32[3,16,4,1]{3,1,2,0:T(8,128)S(1)} %get-tuple-element.950), channel_id=1, source_target_pairs={{0,2},{1,3},{4,6},{5,7},{8,10},{9,11},{12,14},{13,15},{16,18},{17,... | collective-permute-start | bytes 2312 | tf_op jit(solution)/shard_map/ppermute | solution.py:19
  136.1 13.7 %collective-permute-start.11 = (f32[3,1,4,130]{3,1,2,0:T(1,128)S(1)}, f32[3,1,4,130]{3,1,2,0:T(1,128)S(1)}, u32[]{:S(2)}, u32[]{:S(2)}) collective-permute-start(f32[3,1,4,130]{3,1,2,0:T(1,128)S(1)} %get-tuple-element.799), channel_id=1, source_target_pairs={{0,1},{2,3},{4,5},{6,7},{8,9},{10,11},{12,13},{14,15},{16,17},{18,... | collective-permute-start | bytes 18728 | tf_op jit(solution)/shard_map/ppermute | solution.py:19
  140.8 13.4 %collective-permute-start.35 = (f32[3,1,4,130]{3,1,2,0:T(1,128)S(1)}, f32[3,1,4,130]{3,1,2,0:T(1,128)S(1)}, u32[]{:S(2)}, u32[]{:S(2)}) collective-permute-start(f32[3,1,4,130]{3,1,2,0:T(1,128)S(1)} %get-tuple-element.803), channel_id=1, source_target_pairs={{0,1},{2,3},{4,5},{6,7},{8,9},{10,11},{12,13},{14,15},{16,17},{18,... | collective-permute-start | bytes 18728 | tf_op jit(solution)/shard_map/ppermute | solution.py:19
  158.1 15.8 %collective-permute-start.14 = (f32[3,16,128]{2,1,0:T(8,128)S(1)}, f32[3,16,128]{2,1,0:T(8,128)S(1)}, u32[]{:S(2)}, u32[]{:S(2)}) collective-permute-start(f32[3,16,128]{2,1,0:T(8,128)S(1)} %get-tuple-element.795), channel_id=1, source_target_pairs={{4,0},{8,4},{12,8},{5,1},{9,5},{13,9},{6,2},{10,6},{14,10},{7,3},{... | collective-permute-start | bytes 73736 | tf_op jit(solution)/shard_map/ppermute | solution.py:28
  159.4 14.3 %collective-permute-start.12 = (f32[3,2,128]{2,1,0:T(2,128)S(1)}, f32[3,2,128]{2,1,0:T(2,128)S(1)}, u32[]{:S(2)}, u32[]{:S(2)}) collective-permute-start(f32[3,2,128]{2,1,0:T(2,128)S(1)} %bitcast.1244), channel_id=1, source_target_pairs={{1,0},{3,2},{5,4},{7,6},{9,8},{11,10},{13,12},{15,14},{17,16},{19,... | collective-permute-start | bytes 9224 | tf_op jit(solution)/shard_map/ppermute | solution.py:28
  160.7 12.9 %collective-permute-start.17 = (f32[3,16,2]{1,2,0:T(2,128)S(1)}, f32[3,16,2]{1,2,0:T(2,128)S(1)}, u32[]{:S(2)}, u32[]{:S(2)}) collective-permute-start(f32[3,16,2]{1,2,0:T(2,128)S(1)} %get-tuple-element.662), channel_id=1, source_target_pairs={{0,2},{1,3},{4,6},{5,7},{8,10},{9,11},{12,14},{13,15},{16,18},{17,... | collective-permute-start | bytes 1160 | tf_op jit(solution)/shard_map/ppermute | solution.py:28
  177.0 16.3 %collective-permute-start.18 = (f32[3,2,128]{2,1,0:T(2,128)S(1)}, f32[3,2,128]{2,1,0:T(2,128)S(1)}, u32[]{:S(2)}, u32[]{:S(2)}) collective-permute-start(f32[3,2,128]{2,1,0:T(2,128)S(1)} %bitcast.1241), channel_id=1, source_target_pairs={{1,0},{3,2},{5,4},{7,6},{9,8},{11,10},{13,12},{15,14},{17,16},{19,... | collective-permute-start | bytes 9224 | tf_op jit(solution)/shard_map/ppermute | solution.py:28
  179.7 13.7 %collective-permute-start.20 = (f32[3,16,128]{2,1,0:T(8,128)S(1)}, f32[3,16,128]{2,1,0:T(8,128)S(1)}, u32[]{:S(2)}, u32[]{:S(2)}) collective-permute-start(f32[3,16,128]{2,1,0:T(8,128)S(1)} %get-tuple-element.790), channel_id=1, source_target_pairs={{4,0},{8,4},{12,8},{5,1},{9,5},{13,9},{6,2},{10,6},{14,10},{7,3},{... | collective-permute-start | bytes 73736 | tf_op jit(solution)/shard_map/ppermute | solution.py:28
  181.1 12.0 %collective-permute-start.23 = (f32[3,16,2]{1,2,0:T(2,128)S(1)}, f32[3,16,2]{1,2,0:T(2,128)S(1)}, u32[]{:S(2)}, u32[]{:S(2)}) collective-permute-start(f32[3,16,2]{1,2,0:T(2,128)S(1)} %get-tuple-element.660), channel_id=1, source_target_pairs={{0,2},{1,3},{4,6},{5,7},{8,10},{9,11},{12,14},{13,15},{16,18},{17,... | collective-permute-start | bytes 1160 | tf_op jit(solution)/shard_map/ppermute | solution.py:28
  196.4 16.7 %collective-permute-start.36 = (f32[3,2,128]{2,1,0:T(2,128)S(1)}, f32[3,2,128]{2,1,0:T(2,128)S(1)}, u32[]{:S(2)}, u32[]{:S(2)}) collective-permute-start(f32[3,2,128]{2,1,0:T(2,128)S(1)} %bitcast.1268), channel_id=1, source_target_pairs={{1,0},{3,2},{5,4},{7,6},{9,8},{11,10},{13,12},{15,14},{17,16},{19,... | collective-permute-start | bytes 9224 | tf_op jit(solution)/shard_map/ppermute | solution.py:28
  199.3 13.9 %collective-permute-start.37 = (f32[3,2,128]{2,1,0:T(2,128)S(1)}, f32[3,2,128]{2,1,0:T(2,128)S(1)}, u32[]{:S(2)}, u32[]{:S(2)}) collective-permute-start(f32[3,2,128]{2,1,0:T(2,128)S(1)} %bitcast.1271), channel_id=1, source_target_pairs={{0,1},{2,3},{4,5},{6,7},{8,9},{10,11},{12,13},{14,15},{16,17},{18,... | collective-permute-start | bytes 9224 | tf_op jit(solution)/shard_map/ppermute | solution.py:28
  216.3 16.3 %collective-permute-start.42 = (f32[3,2,128]{2,1,0:T(2,128)S(1)}, f32[3,2,128]{2,1,0:T(2,128)S(1)}, u32[]{:S(2)}, u32[]{:S(2)}) collective-permute-start(f32[3,2,128]{2,1,0:T(2,128)S(1)} %bitcast.1242), channel_id=1, source_target_pairs={{1,0},{3,2},{5,4},{7,6},{9,8},{11,10},{13,12},{15,14},{17,16},{19,... | collective-permute-start | bytes 9224 | tf_op jit(solution)/shard_map/ppermute | solution.py:28
  219.0 13.7 %collective-permute-start.44 = (f32[3,16,128]{2,1,0:T(8,128)S(1)}, f32[3,16,128]{2,1,0:T(8,128)S(1)}, u32[]{:S(2)}, u32[]{:S(2)}) collective-permute-start(f32[3,16,128]{2,1,0:T(8,128)S(1)} %get-tuple-element.779), channel_id=1, source_target_pairs={{4,0},{8,4},{12,8},{5,1},{9,5},{13,9},{6,2},{10,6},{14,10},{7,3},{... | collective-permute-start | bytes 73736 | tf_op jit(solution)/shard_map/ppermute | solution.py:28
  235.7 16.7 %collective-permute-start.60 = (f32[3,2,128]{2,1,0:T(2,128)S(1)}, f32[3,2,128]{2,1,0:T(2,128)S(1)}, u32[]{:S(2)}, u32[]{:S(2)}) collective-permute-start(f32[3,2,128]{2,1,0:T(2,128)S(1)} %bitcast.1269), channel_id=1, source_target_pairs={{1,0},{3,2},{5,4},{7,6},{9,8},{11,10},{13,12},{15,14},{17,16},{19,... | collective-permute-start | bytes 9224 | tf_op jit(solution)/shard_map/ppermute | solution.py:28
  238.6 13.9 %collective-permute-start.61 = (f32[3,2,128]{2,1,0:T(2,128)S(1)}, f32[3,2,128]{2,1,0:T(2,128)S(1)}, u32[]{:S(2)}, u32[]{:S(2)}) collective-permute-start(f32[3,2,128]{2,1,0:T(2,128)S(1)} %bitcast.1272), channel_id=1, source_target_pairs={{0,1},{2,3},{4,5},{6,7},{8,9},{10,11},{12,13},{14,15},{16,17},{18,... | collective-permute-start | bytes 9224 | tf_op jit(solution)/shard_map/ppermute | solution.py:28
  255.5 16.3 %collective-permute-start.66 = (f32[3,2,128]{2,1,0:T(2,128)S(1)}, f32[3,2,128]{2,1,0:T(2,128)S(1)}, u32[]{:S(2)}, u32[]{:S(2)}) collective-permute-start(f32[3,2,128]{2,1,0:T(2,128)S(1)} %bitcast.1243), channel_id=1, source_target_pairs={{1,0},{3,2},{5,4},{7,6},{9,8},{11,10},{13,12},{15,14},{17,16},{19,... | collective-permute-start | bytes 9224 | tf_op jit(solution)/shard_map/ppermute | solution.py:28
  258.3 13.7 %collective-permute-start.68 = (f32[3,16,128]{2,1,0:T(8,128)S(1)}, f32[3,16,128]{2,1,0:T(8,128)S(1)}, u32[]{:S(2)}, u32[]{:S(2)}) collective-permute-start(f32[3,16,128]{2,1,0:T(8,128)S(1)} %get-tuple-element.768), channel_id=1, source_target_pairs={{4,0},{8,4},{12,8},{5,1},{9,5},{13,9},{6,2},{10,6},{14,10},{7,3},{... | collective-permute-start | bytes 73736 | tf_op jit(solution)/shard_map/ppermute | solution.py:28
  275.0 16.7 %collective-permute-start.84 = (f32[3,2,128]{2,1,0:T(2,128)S(1)}, f32[3,2,128]{2,1,0:T(2,128)S(1)}, u32[]{:S(2)}, u32[]{:S(2)}) collective-permute-start(f32[3,2,128]{2,1,0:T(2,128)S(1)} %bitcast.1270), channel_id=1, source_target_pairs={{1,0},{3,2},{5,4},{7,6},{9,8},{11,10},{13,12},{15,14},{17,16},{19,... | collective-permute-start | bytes 9224 | tf_op jit(solution)/shard_map/ppermute | solution.py:28
  277.9 13.9 %collective-permute-start.85 = (f32[3,2,128]{2,1,0:T(2,128)S(1)}, f32[3,2,128]{2,1,0:T(2,128)S(1)}, u32[]{:S(2)}, u32[]{:S(2)}) collective-permute-start(f32[3,2,128]{2,1,0:T(2,128)S(1)} %bitcast.1273), channel_id=1, source_target_pairs={{0,1},{2,3},{4,5},{6,7},{8,9},{10,11},{12,13},{14,15},{16,17},{18,... | collective-permute-start | bytes 9224 | tf_op jit(solution)/shard_map/ppermute | solution.py:28
  317.0 15.7 %collective-permute-start.90 = (f32[3,2,128]{2,1,0:T(2,128)S(1)}, f32[3,2,128]{2,1,0:T(2,128)S(1)}, u32[]{:S(2)}, u32[]{:S(2)}) collective-permute-start(f32[3,2,128]{2,1,0:T(2,128)S(1)} %bitcast.1236), channel_id=1, source_target_pairs={{1,0},{3,2},{5,4},{7,6},{9,8},{11,10},{13,12},{15,14},{17,16},{19,... | collective-permute-start | bytes 9224 | tf_op jit(solution)/shard_map/ppermute | solution.py:28
  319.8 13.1 %collective-permute-start.92 = (f32[3,16,128]{2,1,0:T(8,128)S(1)}, f32[3,16,128]{2,1,0:T(8,128)S(1)}, u32[]{:S(2)}, u32[]{:S(2)}) collective-permute-start(f32[3,16,128]{2,1,0:T(8,128)S(1)} %get-tuple-element.757), channel_id=1, source_target_pairs={{4,0},{8,4},{12,8},{5,1},{9,5},{13,9},{6,2},{10,6},{14,10},{7,3},{... | collective-permute-start | bytes 73736 | tf_op jit(solution)/shard_map/ppermute | solution.py:28
  (53 other events, 427.7 us)
where the time goes:
time: 338 us; the launch traced here: 335 us
  starting transfers between devices  253 us (75%)
  waiting for transfers between devices  21.6 us (6%)
  blocking collectives  21.1 us (6%)
  local copies, waits for them, and re-layouts  18.6 us (6%)
  other arithmetic  17.4 us (5%)
  between operations  3.73 us (1%)
    ppermute x48, starting transfers between devices, passed_along(): return lax.ppermute(block, axis, route)  127 us
    ppermute x24, starting transfers between devices, with_halo(): before = lax.ppermute(last, axis, up)  90.8 us
    ppermute x24, starting transfers between devices, with_halo(): after = lax.ppermute(initial, axis, down)  31 us
    psum x1, blocking collectives, on_device(): summed_drag, summed_cost = lax.psum((seg_drag, seg_cost), ('gx', 'col'))  21.1 us
    ppermute x24, waiting for transfers between devices, with_halo(): after = lax.ppermute(initial, axis, down)  9.11 us
    ppermute x48, waiting for transfers between devices, passed_along(): return lax.ppermute(block, axis, route)  8.69 us
    unnamed x16, local copies, waits for them, and re-layouts  7.13 us
  transfers between devices with their start and end apart: 97, of which 14 were waited for; matrix products, arithmetic and copies ran while one was open for 3% of the time, Pallas kernels for 0%

commit v1 on v0

--- a/solution.py
+++ b/solution.py
@@ -141,7 +141,7 @@
             cot_pad, cot_drag = pull(adjoint)
             seg_drag = seg_drag + cot_drag
             adjoint = halo_back(cot_pad)
-        summed_drag, summed_cost = lax.psum((seg_drag, seg_cost), ("gx", "col"))
+        summed_drag, summed_cost = lax.psum(lax.psum((seg_drag, seg_cost), "col"), "gx")
         drag_total = drag_total + summed_drag
         cost = cost + summed_cost
     scale = 1.0 / (total_lat * total_lon)

time: 338 us -> 335 us (level)
    psum x1 -> x2, blocking collectives: 21.1 us -> 18.5 us  [the longest x1 13.5 us: on_device(): lax.psum(lax.psum((seg_drag, seg_cost), 'col'), 'gx')]
where the time goes in v1:
time: 335 us; the launch traced here: 333 us
  starting transfers between devices  253 us (76%)
  waiting for transfers between devices  21.6 us (6%)
  local copies, waits for them, and re-layouts  18.6 us (6%)
  blocking collectives  18.5 us (6%)
  other arithmetic  17.4 us (5%)
  between operations  3.73 us (1%)
    ppermute x48, starting transfers between devices, passed_along(): return lax.ppermute(block, axis, route)  127 us
    ppermute x24, starting transfers between devices, with_halo(): before = lax.ppermute(last, axis, up)  90.8 us
    ppermute x24, starting transfers between devices, with_halo(): after = lax.ppermute(initial, axis, down)  31 us
    psum x1, blocking collectives, on_device(): lax.psum(lax.psum((seg_drag, seg_cost), 'col'), 'gx')  13.5 us
    ppermute x24, waiting for transfers between devices, with_halo(): after = lax.ppermute(initial, axis, down)  9.11 us
    ppermute x48, waiting for transfers between devices, passed_along(): return lax.ppermute(block, axis, route)  8.69 us
    unnamed x16, local copies, waits for them, and re-layouts  7.13 us
  transfers between devices with their start and end apart: 97, of which 14 were waited for; matrix products, arithmetic and copies ran while one was open for 3% of the time, Pallas kernels for 0%

profile of v1, /device:TPU:0, one launch (start us, length us, event | category | flops | bytes accessed | tf_op | source)
XLA Modules:
  0.0 332.7 jit_solution(13157739534137440349)
XLA Ops:
  4.4 4.4 %all-to-all-start = ((bf16[2,2,12288]{2,1,0:T(2,128)(2,1)}), bf16[2,2,12288]{2,1,0:T(2,128)(2,1)S(1)}, u32[]{:S(2)}, u32[]{:S(2)}) async-start(bf16[2,2,12288]{2,1,0:T(2,128)(2,1)} %reshape.2001), calls=%async_computation | async-start | bytes 196608 | tf_op jit(solution)/shard_map/all_to_all | solution.py:118
  10.6 2.6 all-to-all-done
  14.7 4.0 %collective-permute-start = (f32[3,16,1,128]{3,1,2,0:T(8,128)S(1)}, f32[3,16,1,128]{3,1,2,0:T(8,128)S(1)}, u32[]{:S(2)}, u32[]{:S(2)}) collective-permute-start(f32[3,16,1,128]{3,1,2,0:T(8,128)S(1)} %get-tuple-element.1055), channel_id=1, source_target_pairs={{0,4},{4,8},{8,12},{1,5},{5,9},{9,13},{2,6},{6,10},{10,14},{3,7},{... | collective-permute-start | bytes 73736 | tf_op jit(solution)/shard_map/ppermute | solution.py:19
  20.0 4.5 %collective-permute-start.24 = (f32[3,16,1,128]{3,1,2,0:T(8,128)S(1)}, f32[3,16,1,128]{3,1,2,0:T(8,128)S(1)}, u32[]{:S(2)}, u32[]{:S(2)}) collective-permute-start(f32[3,16,1,128]{3,1,2,0:T(8,128)S(1)} %get-tuple-element.1059), channel_id=1, source_target_pairs={{0,4},{4,8},{8,12},{1,5},{5,9},{9,13},{2,6},{6,10},{10,14},{3,7},{... | collective-permute-start | bytes 73736 | tf_op jit(solution)/shard_map/ppermute | solution.py:19
  25.9 4.5 %collective-permute-start.48 = (f32[3,16,1,128]{3,1,2,0:T(8,128)S(1)}, f32[3,16,1,128]{3,1,2,0:T(8,128)S(1)}, u32[]{:S(2)}, u32[]{:S(2)}) collective-permute-start(f32[3,16,1,128]{3,1,2,0:T(8,128)S(1)} %get-tuple-element.1063), channel_id=1, source_target_pairs={{0,4},{4,8},{8,12},{1,5},{5,9},{9,13},{2,6},{6,10},{10,14},{3,7},{... | collective-permute-start | bytes 73736 | tf_op jit(solution)/shard_map/ppermute | solution.py:19
  31.8 4.5 %collective-permute-start.72 = (f32[3,16,1,128]{3,1,2,0:T(8,128)S(1)}, f32[3,16,1,128]{3,1,2,0:T(8,128)S(1)}, u32[]{:S(2)}, u32[]{:S(2)}) collective-permute-start(f32[3,16,1,128]{3,1,2,0:T(8,128)S(1)} %get-tuple-element.1067), channel_id=1, source_target_pairs={{0,4},{4,8},{8,12},{1,5},{5,9},{9,13},{2,6},{6,10},{10,14},{3,7},{... | collective-permute-start | bytes 73736 | tf_op jit(solution)/shard_map/ppermute | solution.py:19
  41.1 4.6 %collective-permute-start.26 = (f32[3,16,4,1]{3,1,2,0:T(8,128)S(1)}, f32[3,16,4,1]{3,1,2,0:T(8,128)S(1)}, u32[]{:S(2)}, u32[]{:S(2)}) collective-permute-start(f32[3,16,4,1]{3,1,2,0:T(8,128)S(1)} %get-tuple-element.950), channel_id=1, source_target_pairs={{0,2},{1,3},{4,6},{5,7},{8,10},{9,11},{12,14},{13,15},{16,18},{17,... | collective-permute-start | bytes 2312 | tf_op jit(solution)/shard_map/ppermute | solution.py:19
  47.1 4.6 %collective-permute-start.50 = (f32[3,16,4,1]{3,1,2,0:T(8,128)S(1)}, f32[3,16,4,1]{3,1,2,0:T(8,128)S(1)}, u32[]{:S(2)}, u32[]{:S(2)}) collective-permute-start(f32[3,16,4,1]{3,1,2,0:T(8,128)S(1)} %get-tuple-element.954), channel_id=1, source_target_pairs={{0,2},{1,3},{4,6},{5,7},{8,10},{9,11},{12,14},{13,15},{16,18},{17,... | collective-permute-start | bytes 2312 | tf_op jit(solution)/shard_map/ppermute | solution.py:19
  53.1 4.6 %collective-permute-start.74 = (f32[3,16,4,1]{3,1,2,0:T(8,128)S(1)}, f32[3,16,4,1]{3,1,2,0:T(8,128)S(1)}, u32[]{:S(2)}, u32[]{:S(2)}) collective-permute-start(f32[3,16,4,1]{3,1,2,0:T(8,128)S(1)} %get-tuple-element.958), channel_id=1, source_target_pairs={{0,2},{1,3},{4,6},{5,7},{8,10},{9,11},{12,14},{13,15},{16,18},{17,... | collective-permute-start | bytes 2312 | tf_op jit(solution)/shard_map/ppermute | solution.py:19
  59.8 4.5 %collective-permute-done.75 = f32[3,16,4,1]{3,1,2,0:T(8,128)S(1)} collective-permute-done((f32[3,16,4,1]{3,1,2,0:T(8,128)S(1)}, f32[3,16,4,1]{3,1,2,0:T(8,128)S(1)}, u32[]{:S(2)}, u32[]{:S(2)}) %collective-permute-start.75) | collective-permute-done | bytes 800 | tf_op jit(solution)/shard_map/ppermute | solution.py:20
  66.2 3.0 collective-permute-start.5
  70.9 3.0 collective-permute-start.29
  76.5 3.0 collective-permute-start.53
  81.0 3.0 collective-permute-start.77
  84.0 4.5 %collective-permute-start.6 = (f32[3,16,1,128]{3,1,2,0:T(8,128)S(1)}, f32[3,16,1,128]{3,1,2,0:T(8,128)S(1)}, u32[]{:S(2)}, u32[]{:S(2)}) collective-permute-start(f32[3,16,1,128]{3,1,2,0:T(8,128)S(1)} %get-tuple-element.1053), channel_id=1, source_target_pairs={{0,4},{4,8},{8,12},{1,5},{5,9},{9,13},{2,6},{6,10},{10,14},{3,7},{... | collective-permute-start | bytes 73736 | tf_op jit(solution)/shard_map/ppermute | solution.py:19
  90.0 4.5 %collective-permute-start.30 = (f32[3,16,1,128]{3,1,2,0:T(8,128)S(1)}, f32[3,16,1,128]{3,1,2,0:T(8,128)S(1)}, u32[]{:S(2)}, u32[]{:S(2)}) collective-permute-start(f32[3,16,1,128]{3,1,2,0:T(8,128)S(1)} %get-tuple-element.1057), channel_id=1, source_target_pairs={{0,4},{4,8},{8,12},{1,5},{5,9},{9,13},{2,6},{6,10},{10,14},{3,7},{... | collective-permute-start | bytes 73736 | tf_op jit(solution)/shard_map/ppermute | solution.py:19
  96.0 4.5 %collective-permute-start.54 = (f32[3,16,1,128]{3,1,2,0:T(8,128)S(1)}, f32[3,16,1,128]{3,1,2,0:T(8,128)S(1)}, u32[]{:S(2)}, u32[]{:S(2)}) collective-permute-start(f32[3,16,1,128]{3,1,2,0:T(8,128)S(1)} %get-tuple-element.1061), channel_id=1, source_target_pairs={{0,4},{4,8},{8,12},{1,5},{5,9},{9,13},{2,6},{6,10},{10,14},{3,7},{... | collective-permute-start | bytes 73736 | tf_op jit(solution)/shard_map/ppermute | solution.py:19
  102.0 4.5 %collective-permute-start.78 = (f32[3,16,1,128]{3,1,2,0:T(8,128)S(1)}, f32[3,16,1,128]{3,1,2,0:T(8,128)S(1)}, u32[]{:S(2)}, u32[]{:S(2)}) collective-permute-start(f32[3,16,1,128]{3,1,2,0:T(8,128)S(1)} %get-tuple-element.1065), channel_id=1, source_target_pairs={{0,4},{4,8},{8,12},{1,5},{5,9},{9,13},{2,6},{6,10},{10,14},{3,7},{... | collective-permute-start | bytes 73736 | tf_op jit(solution)/shard_map/ppermute | solution.py:19
  111.0 4.6 %collective-permute-start.32 = (f32[3,16,4,1]{3,1,2,0:T(8,128)S(1)}, f32[3,16,4,1]{3,1,2,0:T(8,128)S(1)}, u32[]{:S(2)}, u32[]{:S(2)}) collective-permute-start(f32[3,16,4,1]{3,1,2,0:T(8,128)S(1)} %get-tuple-element.948), channel_id=1, source_target_pairs={{0,2},{1,3},{4,6},{5,7},{8,10},{9,11},{12,14},{13,15},{16,18},{17,... | collective-permute-start | bytes 2312 | tf_op jit(solution)/shard_map/ppermute | solution.py:19
  117.0 4.6 %collective-permute-start.56 = (f32[3,16,4,1]{3,1,2,0:T(8,128)S(1)}, f32[3,16,4,1]{3,1,2,0:T(8,128)S(1)}, u32[]{:S(2)}, u32[]{:S(2)}) collective-permute-start(f32[3,16,4,1]{3,1,2,0:T(8,128)S(1)} %get-tuple-element.952), channel_id=1, source_target_pairs={{0,2},{1,3},{4,6},{5,7},{8,10},{9,11},{12,14},{13,15},{16,18},{17,... | collective-permute-start | bytes 2312 | tf_op jit(solution)/shard_map/ppermute | solution.py:19
  122.9 4.6 %collective-permute-start.80 = (f32[3,16,4,1]{3,1,2,0:T(8,128)S(1)}, f32[3,16,4,1]{3,1,2,0:T(8,128)S(1)}, u32[]{:S(2)}, u32[]{:S(2)}) collective-permute-start(f32[3,16,4,1]{3,1,2,0:T(8,128)S(1)} %get-tuple-element.956), channel_id=1, source_target_pairs={{0,2},{1,3},{4,6},{5,7},{8,10},{9,11},{12,14},{13,15},{16,18},{17,... | collective-permute-start | bytes 2312 | tf_op jit(solution)/shard_map/ppermute | solution.py:19
  129.7 4.5 %collective-permute-done.81 = f32[3,16,4,1]{3,1,2,0:T(8,128)S(1)} collective-permute-done((f32[3,16,4,1]{3,1,2,0:T(8,128)S(1)}, f32[3,16,4,1]{3,1,2,0:T(8,128)S(1)}, u32[]{:S(2)}, u32[]{:S(2)}) %collective-permute-start.81) | collective-permute-done | bytes 800 | tf_op jit(solution)/shard_map/ppermute | solution.py:20
  136.1 3.0 collective-permute-start.11
  140.8 3.0 collective-permute-start.35
  146.8 3.0 collective-permute-start.59
  151.2 3.0 collective-permute-start.83
  160.7 4.5 %collective-permute-start.17 = (f32[3,16,2]{1,2,0:T(2,128)S(1)}, f32[3,16,2]{1,2,0:T(2,128)S(1)}, u32[]{:S(2)}, u32[]{:S(2)}) collective-permute-start(f32[3,16,2]{1,2,0:T(2,128)S(1)} %get-tuple-element.662), channel_id=1, source_target_pairs={{0,2},{1,3},{4,6},{5,7},{8,10},{9,11},{12,14},{13,15},{16,18},{17,... | collective-permute-start | bytes 1160 | tf_op jit(solution)/shard_map/ppermute | solution.py:28
  165.5 2.7 collective-permute-start.13
  168.2 5.2 %collective-permute-start.15 = (f32[3,16,128]{2,1,0:T(8,128)S(1)}, f32[3,16,128]{2,1,0:T(8,128)S(1)}, u32[]{:S(2)}, u32[]{:S(2)}) collective-permute-start(f32[3,16,128]{2,1,0:T(8,128)S(1)} %get-tuple-element.796), channel_id=1, source_target_pairs={{0,4},{4,8},{8,12},{1,5},{5,9},{9,13},{2,6},{6,10},{10,14},{3,7},{... | collective-permute-start | bytes 73736 | tf_op jit(solution)/shard_map/ppermute | solution.py:28
  181.1 4.5 %collective-permute-start.23 = (f32[3,16,2]{1,2,0:T(2,128)S(1)}, f32[3,16,2]{1,2,0:T(2,128)S(1)}, u32[]{:S(2)}, u32[]{:S(2)}) collective-permute-start(f32[3,16,2]{1,2,0:T(2,128)S(1)} %get-tuple-element.660), channel_id=1, source_target_pairs={{0,2},{1,3},{4,6},{5,7},{8,10},{9,11},{12,14},{13,15},{16,18},{17,... | collective-permute-start | bytes 1160 | tf_op jit(solution)/shard_map/ppermute | solution.py:28
  188.2 4.8 %collective-permute-start.21 = (f32[3,16,128]{2,1,0:T(8,128)S(1)}, f32[3,16,128]{2,1,0:T(8,128)S(1)}, u32[]{:S(2)}, u32[]{:S(2)}) collective-permute-start(f32[3,16,128]{2,1,0:T(8,128)S(1)} %get-tuple-element.791), channel_id=1, source_target_pairs={{0,4},{4,8},{8,12},{1,5},{5,9},{9,13},{2,6},{6,10},{10,14},{3,7},{... | collective-permute-start | bytes 73736 | tf_op jit(solution)/shard_map/ppermute | solution.py:28
  199.3 3.0 collective-permute-start.37
  202.4 4.3 %collective-permute-start.41 = (f32[3,16,2]{1,2,0:T(2,128)S(1)}, f32[3,16,2]{1,2,0:T(2,128)S(1)}, u32[]{:S(2)}, u32[]{:S(2)}) collective-permute-start(f32[3,16,2]{1,2,0:T(2,128)S(1)} %bitcast.1257), channel_id=1, source_target_pairs={{0,2},{1,3},{4,6},{5,7},{8,10},{9,11},{12,14},{13,15},{16,18},{17,... | collective-permute-start | bytes 1160 | tf_op jit(solution)/shard_map/ppermute | solution.py:28
  208.0 4.8 %collective-permute-start.39 = (f32[3,16,128]{2,1,0:T(8,128)S(1)}, f32[3,16,128]{2,1,0:T(8,128)S(1)}, u32[]{:S(2)}, u32[]{:S(2)}) collective-permute-start(f32[3,16,128]{2,1,0:T(8,128)S(1)} %get-tuple-element.787), channel_id=1, source_target_pairs={{0,4},{4,8},{8,12},{1,5},{5,9},{9,13},{2,6},{6,10},{10,14},{3,7},{... | collective-permute-start | bytes 73736 | tf_op jit(solution)/shard_map/ppermute | solution.py:28
  220.4 4.5 %collective-permute-start.47 = (f32[3,16,2]{1,2,0:T(2,128)S(1)}, f32[3,16,2]{1,2,0:T(2,128)S(1)}, u32[]{:S(2)}, u32[]{:S(2)}) collective-permute-start(f32[3,16,2]{1,2,0:T(2,128)S(1)} %get-tuple-element.658), channel_id=1, source_target_pairs={{0,2},{1,3},{4,6},{5,7},{8,10},{9,11},{12,14},{13,15},{16,18},{17,... | collective-permute-start | bytes 1160 | tf_op jit(solution)/shard_map/ppermute | solution.py:28
  227.5 4.8 %collective-permute-start.45 = (f32[3,16,128]{2,1,0:T(8,128)S(1)}, f32[3,16,128]{2,1,0:T(8,128)S(1)}, u32[]{:S(2)}, u32[]{:S(2)}) collective-permute-start(f32[3,16,128]{2,1,0:T(8,128)S(1)} %get-tuple-element.780), channel_id=1, source_target_pairs={{0,4},{4,8},{8,12},{1,5},{5,9},{9,13},{2,6},{6,10},{10,14},{3,7},{... | collective-permute-start | bytes 73736 | tf_op jit(solution)/shard_map/ppermute | solution.py:28
  238.6 3.0 collective-permute-start.61
  241.7 4.3 %collective-permute-start.65 = (f32[3,16,2]{1,2,0:T(2,128)S(1)}, f32[3,16,2]{1,2,0:T(2,128)S(1)}, u32[]{:S(2)}, u32[]{:S(2)}) collective-permute-start(f32[3,16,2]{1,2,0:T(2,128)S(1)} %bitcast.1261), channel_id=1, source_target_pairs={{0,2},{1,3},{4,6},{5,7},{8,10},{9,11},{12,14},{13,15},{16,18},{17,... | collective-permute-start | bytes 1160 | tf_op jit(solution)/shard_map/ppermute | solution.py:28
  247.3 4.8 %collective-permute-start.63 = (f32[3,16,128]{2,1,0:T(8,128)S(1)}, f32[3,16,128]{2,1,0:T(8,128)S(1)}, u32[]{:S(2)}, u32[]{:S(2)}) collective-permute-start(f32[3,16,128]{2,1,0:T(8,128)S(1)} %get-tuple-element.776), channel_id=1, source_target_pairs={{0,4},{4,8},{8,12},{1,5},{5,9},{9,13},{2,6},{6,10},{10,14},{3,7},{... | collective-permute-start | bytes 73736 | tf_op jit(solution)/shard_map/ppermute | solution.py:28
  259.7 4.5 %collective-permute-start.71 = (f32[3,16,2]{1,2,0:T(2,128)S(1)}, f32[3,16,2]{1,2,0:T(2,128)S(1)}, u32[]{:S(2)}, u32[]{:S(2)}) collective-permute-start(f32[3,16,2]{1,2,0:T(2,128)S(1)} %get-tuple-element.656), channel_id=1, source_target_pairs={{0,2},{1,3},{4,6},{5,7},{8,10},{9,11},{12,14},{13,15},{16,18},{17,... | collective-permute-start | bytes 1160 | tf_op jit(solution)/shard_map/ppermute | solution.py:28
  266.7 4.8 %collective-permute-start.69 = (f32[3,16,128]{2,1,0:T(8,128)S(1)}, f32[3,16,128]{2,1,0:T(8,128)S(1)}, u32[]{:S(2)}, u32[]{:S(2)}) collective-permute-start(f32[3,16,128]{2,1,0:T(8,128)S(1)} %get-tuple-element.769), channel_id=1, source_target_pairs={{0,4},{4,8},{8,12},{1,5},{5,9},{9,13},{2,6},{6,10},{10,14},{3,7},{... | collective-permute-start | bytes 73736 | tf_op jit(solution)/shard_map/ppermute | solution.py:28
  277.9 3.0 collective-permute-start.85
  281.0 4.3 %collective-permute-start.89 = (f32[3,16,2]{1,2,0:T(2,128)S(1)}, f32[3,16,2]{1,2,0:T(2,128)S(1)}, u32[]{:S(2)}, u32[]{:S(2)}) collective-permute-start(f32[3,16,2]{1,2,0:T(2,128)S(1)} %bitcast.1265), channel_id=1, source_target_pairs={{0,2},{1,3},{4,6},{5,7},{8,10},{9,11},{12,14},{13,15},{16,18},{17,... | collective-permute-start | bytes 1160 | tf_op jit(solution)/shard_map/ppermute | solution.py:28
  286.6 4.8 %collective-permute-start.87 = (f32[3,16,128]{2,1,0:T(8,128)S(1)}, f32[3,16,128]{2,1,0:T(8,128)S(1)}, u32[]{:S(2)}, u32[]{:S(2)}) collective-permute-start(f32[3,16,128]{2,1,0:T(8,128)S(1)} %get-tuple-element.765), channel_id=1, source_target_pairs={{0,4},{4,8},{8,12},{1,5},{5,9},{9,13},{2,6},{6,10},{10,14},{3,7},{... | collective-permute-start | bytes 73736 | tf_op jit(solution)/shard_map/ppermute | solution.py:28
  294.8 4.9 %all-reduce.313 = (f32[16]{0:T(128)S(1)}, f32[16]{0:T(128)S(1)}) all-reduce(f32[16]{0:T(128)S(1)} %add_multiply_fusion, f32[16]{0:T(128)S(1)} %add_add_fusion.1), channel_id=1, replica_groups=mesh['ens'=2,'gx'=4,'col'=2,'gz'=2] {'col'}, use_global_device_ids=true, to_apply=%region_1.0 | all-reduce | flops 32 | bytes 256 | tf_op jit(solution)/shard_map/psum | solution.py:144
  299.8 13.5 %all-reduce.312 = (f32[16]{0:T(128)S(1)}, f32[16]{0:T(128)S(1)}) all-reduce(f32[16]{0:T(128)S(1)} %get-tuple-element.686, f32[16]{0:T(128)S(1)} %get-tuple-element.687), channel_id=1, replica_groups=mesh['ens'=2,'gx'=4,'col'=2,'gz'=2] {'gx'}, use_global_device_ids=true, to_apply=%region_2.0 | all-reduce | flops 32 | bytes 256 | tf_op jit(solution)/shard_map/psum | solution.py:144
  318.5 4.5 %collective-permute-start.95 = (f32[3,16,2]{1,2,0:T(2,128)S(1)}, f32[3,16,2]{1,2,0:T(2,128)S(1)}, u32[]{:S(2)}, u32[]{:S(2)}) collective-permute-start(f32[3,16,2]{1,2,0:T(2,128)S(1)} %get-tuple-element.654), channel_id=1, source_target_pairs={{0,2},{1,3},{4,6},{5,7},{8,10},{9,11},{12,14},{13,15},{16,18},{17,... | collective-permute-start | bytes 1160 | tf_op jit(solution)/shard_map/ppermute | solution.py:28
  325.5 4.3 %collective-permute-start.93 = (f32[3,16,128]{2,1,0:T(8,128)S(1)}, f32[3,16,128]{2,1,0:T(8,128)S(1)}, u32[]{:S(2)}, u32[]{:S(2)}) collective-permute-start(f32[3,16,128]{2,1,0:T(8,128)S(1)} %get-tuple-element.758), channel_id=1, source_target_pairs={{0,4},{4,8},{8,12},{1,5},{5,9},{9,13},{2,6},{6,10},{10,14},{3,7},{... | collective-permute-start | bytes 73736 | tf_op jit(solution)/shard_map/ppermute | solution.py:28
  (501 shorter events, 121.3 us)
Async XLA Ops:
  14.7 15.8 %collective-permute-start = (f32[3,16,1,128]{3,1,2,0:T(8,128)S(1)}, f32[3,16,1,128]{3,1,2,0:T(8,128)S(1)}, u32[]{:S(2)}, u32[]{:S(2)}) collective-permute-start(f32[3,16,1,128]{3,1,2,0:T(8,128)S(1)} %get-tuple-element.1055), channel_id=1, source_target_pairs={{0,4},{4,8},{8,12},{1,5},{5,9},{9,13},{2,6},{6,10},{10,14},{3,7},{... | collective-permute-start | bytes 73736 | tf_op jit(solution)/shard_map/ppermute | solution.py:19
  18.7 13.1 %collective-permute-start.1 = (f32[3,16,1,128]{3,1,2,0:T(8,128)S(1)}, f32[3,16,1,128]{3,1,2,0:T(8,128)S(1)}, u32[]{:S(2)}, u32[]{:S(2)}) collective-permute-start(f32[3,16,1,128]{3,1,2,0:T(8,128)S(1)} %get-tuple-element.1056), channel_id=1, source_target_pairs={{4,0},{8,4},{12,8},{5,1},{9,5},{13,9},{6,2},{10,6},{14,10},{7,3},{... | collective-permute-start | bytes 73736 | tf_op jit(solution)/shard_map/ppermute | solution.py:20
  20.0 16.4 %collective-permute-start.24 = (f32[3,16,1,128]{3,1,2,0:T(8,128)S(1)}, f32[3,16,1,128]{3,1,2,0:T(8,128)S(1)}, u32[]{:S(2)}, u32[]{:S(2)}) collective-permute-start(f32[3,16,1,128]{3,1,2,0:T(8,128)S(1)} %get-tuple-element.1059), channel_id=1, source_target_pairs={{0,4},{4,8},{8,12},{1,5},{5,9},{9,13},{2,6},{6,10},{10,14},{3,7},{... | collective-permute-start | bytes 73736 | tf_op jit(solution)/shard_map/ppermute | solution.py:19
  24.6 13.2 %collective-permute-start.25 = (f32[3,16,1,128]{3,1,2,0:T(8,128)S(1)}, f32[3,16,1,128]{3,1,2,0:T(8,128)S(1)}, u32[]{:S(2)}, u32[]{:S(2)}) collective-permute-start(f32[3,16,1,128]{3,1,2,0:T(8,128)S(1)} %get-tuple-element.1060), channel_id=1, source_target_pairs={{4,0},{8,4},{12,8},{5,1},{9,5},{13,9},{6,2},{10,6},{14,10},{7,3},{... | collective-permute-start | bytes 73736 | tf_op jit(solution)/shard_map/ppermute | solution.py:20
  25.9 13.9 %collective-permute-start.48 = (f32[3,16,1,128]{3,1,2,0:T(8,128)S(1)}, f32[3,16,1,128]{3,1,2,0:T(8,128)S(1)}, u32[]{:S(2)}, u32[]{:S(2)}) collective-permute-start(f32[3,16,1,128]{3,1,2,0:T(8,128)S(1)} %get-tuple-element.1063), channel_id=1, source_target_pairs={{0,4},{4,8},{8,12},{1,5},{5,9},{9,13},{2,6},{6,10},{10,14},{3,7},{... | collective-permute-start | bytes 73736 | tf_op jit(solution)/shard_map/ppermute | solution.py:19
  31.8 14.0 %collective-permute-start.72 = (f32[3,16,1,128]{3,1,2,0:T(8,128)S(1)}, f32[3,16,1,128]{3,1,2,0:T(8,128)S(1)}, u32[]{:S(2)}, u32[]{:S(2)}) collective-permute-start(f32[3,16,1,128]{3,1,2,0:T(8,128)S(1)} %get-tuple-element.1067), channel_id=1, source_target_pairs={{0,4},{4,8},{8,12},{1,5},{5,9},{9,13},{2,6},{6,10},{10,14},{3,7},{... | collective-permute-start | bytes 73736 | tf_op jit(solution)/shard_map/ppermute | solution.py:19
  37.8 14.0 %collective-permute-start.2 = (f32[3,16,4,1]{3,1,2,0:T(8,128)S(1)}, f32[3,16,4,1]{3,1,2,0:T(8,128)S(1)}, u32[]{:S(2)}, u32[]{:S(2)}) collective-permute-start(f32[3,16,4,1]{3,1,2,0:T(8,128)S(1)} %get-tuple-element.946), channel_id=1, source_target_pairs={{0,2},{1,3},{4,6},{5,7},{8,10},{9,11},{12,14},{13,15},{16,18},{17,... | collective-permute-start | bytes 2312 | tf_op jit(solution)/shard_map/ppermute | solution.py:19
  39.8 13.3 %collective-permute-start.3 = (f32[3,16,4,1]{3,1,2,0:T(8,128)S(1)}, f32[3,16,4,1]{3,1,2,0:T(8,128)S(1)}, u32[]{:S(2)}, u32[]{:S(2)}) collective-permute-start(f32[3,16,4,1]{3,1,2,0:T(8,128)S(1)} %get-tuple-element.947), channel_id=1, source_target_pairs={{2,0},{3,1},{6,4},{7,5},{10,8},{11,9},{14,12},{15,13},{18,16},{19,... | collective-permute-start | bytes 2312 | tf_op jit(solution)/shard_map/ppermute | solution.py:20
  41.1 16.7 %collective-permute-start.26 = (f32[3,16,4,1]{3,1,2,0:T(8,128)S(1)}, f32[3,16,4,1]{3,1,2,0:T(8,128)S(1)}, u32[]{:S(2)}, u32[]{:S(2)}) collective-permute-start(f32[3,16,4,1]{3,1,2,0:T(8,128)S(1)} %get-tuple-element.950), channel_id=1, source_target_pairs={{0,2},{1,3},{4,6},{5,7},{8,10},{9,11},{12,14},{13,15},{16,18},{17,... | collective-permute-start | bytes 2312 | tf_op jit(solution)/shard_map/ppermute | solution.py:19
  45.8 13.4 %collective-permute-start.27 = (f32[3,16,4,1]{3,1,2,0:T(8,128)S(1)}, f32[3,16,4,1]{3,1,2,0:T(8,128)S(1)}, u32[]{:S(2)}, u32[]{:S(2)}) collective-permute-start(f32[3,16,4,1]{3,1,2,0:T(8,128)S(1)} %get-tuple-element.951), channel_id=1, source_target_pairs={{2,0},{3,1},{6,4},{7,5},{10,8},{11,9},{14,12},{15,13},{18,16},{19,... | collective-permute-start | bytes 2312 | tf_op jit(solution)/shard_map/ppermute | solution.py:20
  47.1 12.3 %collective-permute-start.50 = (f32[3,16,4,1]{3,1,2,0:T(8,128)S(1)}, f32[3,16,4,1]{3,1,2,0:T(8,128)S(1)}, u32[]{:S(2)}, u32[]{:S(2)}) collective-permute-start(f32[3,16,4,1]{3,1,2,0:T(8,128)S(1)} %get-tuple-element.954), channel_id=1, source_target_pairs={{0,2},{1,3},{4,6},{5,7},{8,10},{9,11},{12,14},{13,15},{16,18},{17,... | collective-permute-start | bytes 2312 | tf_op jit(solution)/shard_map/ppermute | solution.py:19
  66.2 13.3 %collective-permute-start.5 = (f32[3,1,4,130]{3,1,2,0:T(1,128)S(1)}, f32[3,1,4,130]{3,1,2,0:T(1,128)S(1)}, u32[]{:S(2)}, u32[]{:S(2)}) collective-permute-start(f32[3,1,4,130]{3,1,2,0:T(1,128)S(1)} %get-tuple-element.803), channel_id=1, source_target_pairs={{0,1},{2,3},{4,5},{6,7},{8,9},{10,11},{12,13},{14,15},{16,17},{18,... | collective-permute-start | bytes 18728 | tf_op jit(solution)/shard_map/ppermute | solution.py:19
  70.9 13.1 %collective-permute-start.29 = (f32[3,1,4,130]{3,1,2,0:T(1,128)S(1)}, f32[3,1,4,130]{3,1,2,0:T(1,128)S(1)}, u32[]{:S(2)}, u32[]{:S(2)}) collective-permute-start(f32[3,1,4,130]{3,1,2,0:T(1,128)S(1)} %get-tuple-element.807), channel_id=1, source_target_pairs={{0,1},{2,3},{4,5},{6,7},{8,9},{10,11},{12,13},{14,15},{16,17},{18,... | collective-permute-start | bytes 18728 | tf_op jit(solution)/shard_map/ppermute | solution.py:19
  74.3 14.4 %collective-permute-start.52 = (f32[3,1,4,130]{3,1,2,0:T(1,128)S(1)}, f32[3,1,4,130]{3,1,2,0:T(1,128)S(1)}, u32[]{:S(2)}, u32[]{:S(2)}) collective-permute-start(f32[3,1,4,130]{3,1,2,0:T(1,128)S(1)} %get-tuple-element.810), channel_id=1, source_target_pairs={{1,0},{3,2},{5,4},{7,6},{9,8},{11,10},{13,12},{15,14},{17,16},{19,... | collective-permute-start | bytes 18728 | tf_op jit(solution)/shard_map/ppermute | solution.py:20
  76.5 13.5 %collective-permute-start.53 = (f32[3,1,4,130]{3,1,2,0:T(1,128)S(1)}, f32[3,1,4,130]{3,1,2,0:T(1,128)S(1)}, u32[]{:S(2)}, u32[]{:S(2)}) collective-permute-start(f32[3,1,4,130]{3,1,2,0:T(1,128)S(1)} %get-tuple-element.811), channel_id=1, source_target_pairs={{0,1},{2,3},{4,5},{6,7},{8,9},{10,11},{12,13},{14,15},{16,17},{18,... | collective-permute-start | bytes 18728 | tf_op jit(solution)/shard_map/ppermute | solution.py:19
  79.5 15.2 %collective-permute-start.76 = (f32[3,1,4,130]{3,1,2,0:T(1,128)S(1)}, f32[3,1,4,130]{3,1,2,0:T(1,128)S(1)}, u32[]{:S(2)}, u32[]{:S(2)}) collective-permute-start(f32[3,1,4,130]{3,1,2,0:T(1,128)S(1)} %get-tuple-element.814), channel_id=1, source_target_pairs={{1,0},{3,2},{5,4},{7,6},{9,8},{11,10},{13,12},{15,14},{17,16},{19,... | collective-permute-start | bytes 18728 | tf_op jit(solution)/shard_map/ppermute | solution.py:20
  81.0 15.1 %collective-permute-start.77 = (f32[3,1,4,130]{3,1,2,0:T(1,128)S(1)}, f32[3,1,4,130]{3,1,2,0:T(1,128)S(1)}, u32[]{:S(2)}, u32[]{:S(2)}) collective-permute-start(f32[3,1,4,130]{3,1,2,0:T(1,128)S(1)} %get-tuple-element.815), channel_id=1, source_target_pairs={{0,1},{2,3},{4,5},{6,7},{8,9},{10,11},{12,13},{14,15},{16,17},{18,... | collective-permute-start | bytes 18728 | tf_op jit(solution)/shard_map/ppermute | solution.py:19
  84.0 16.7 %collective-permute-start.6 = (f32[3,16,1,128]{3,1,2,0:T(8,128)S(1)}, f32[3,16,1,128]{3,1,2,0:T(8,128)S(1)}, u32[]{:S(2)}, u32[]{:S(2)}) collective-permute-start(f32[3,16,1,128]{3,1,2,0:T(8,128)S(1)} %get-tuple-element.1053), channel_id=1, source_target_pairs={{0,4},{4,8},{8,12},{1,5},{5,9},{9,13},{2,6},{6,10},{10,14},{3,7},{... | collective-permute-start | bytes 73736 | tf_op jit(solution)/shard_map/ppermute | solution.py:19
  88.7 13.3 %collective-permute-start.7 = (f32[3,16,1,128]{3,1,2,0:T(8,128)S(1)}, f32[3,16,1,128]{3,1,2,0:T(8,128)S(1)}, u32[]{:S(2)}, u32[]{:S(2)}) collective-permute-start(f32[3,16,1,128]{3,1,2,0:T(8,128)S(1)} %get-tuple-element.1054), channel_id=1, source_target_pairs={{4,0},{8,4},{12,8},{5,1},{9,5},{13,9},{6,2},{10,6},{14,10},{7,3},{... | collective-permute-start | bytes 73736 | tf_op jit(solution)/shard_map/ppermute | solution.py:20
  90.0 16.7 %collective-permute-start.30 = (f32[3,16,1,128]{3,1,2,0:T(8,128)S(1)}, f32[3,16,1,128]{3,1,2,0:T(8,128)S(1)}, u32[]{:S(2)}, u32[]{:S(2)}) collective-permute-start(f32[3,16,1,128]{3,1,2,0:T(8,128)S(1)} %get-tuple-element.1057), channel_id=1, source_target_pairs={{0,4},{4,8},{8,12},{1,5},{5,9},{9,13},{2,6},{6,10},{10,14},{3,7},{... | collective-permute-start | bytes 73736 | tf_op jit(solution)/shard_map/ppermute | solution.py:19
  94.7 13.3 %collective-permute-start.31 = (f32[3,16,1,128]{3,1,2,0:T(8,128)S(1)}, f32[3,16,1,128]{3,1,2,0:T(8,128)S(1)}, u32[]{:S(2)}, u32[]{:S(2)}) collective-permute-start(f32[3,16,1,128]{3,1,2,0:T(8,128)S(1)} %get-tuple-element.1058), channel_id=1, source_target_pairs={{4,0},{8,4},{12,8},{5,1},{9,5},{13,9},{6,2},{10,6},{14,10},{7,3},{... | collective-permute-start | bytes 73736 | tf_op jit(solution)/shard_map/ppermute | solution.py:20
  96.0 13.6 %collective-permute-start.54 = (f32[3,16,1,128]{3,1,2,0:T(8,128)S(1)}, f32[3,16,1,128]{3,1,2,0:T(8,128)S(1)}, u32[]{:S(2)}, u32[]{:S(2)}) collective-permute-start(f32[3,16,1,128]{3,1,2,0:T(8,128)S(1)} %get-tuple-element.1061), channel_id=1, source_target_pairs={{0,4},{4,8},{8,12},{1,5},{5,9},{9,13},{2,6},{6,10},{10,14},{3,7},{... | collective-permute-start | bytes 73736 | tf_op jit(solution)/shard_map/ppermute | solution.py:19
  102.0 13.6 %collective-permute-start.78 = (f32[3,16,1,128]{3,1,2,0:T(8,128)S(1)}, f32[3,16,1,128]{3,1,2,0:T(8,128)S(1)}, u32[]{:S(2)}, u32[]{:S(2)}) collective-permute-start(f32[3,16,1,128]{3,1,2,0:T(8,128)S(1)} %get-tuple-element.1065), channel_id=1, source_target_pairs={{0,4},{4,8},{8,12},{1,5},{5,9},{9,13},{2,6},{6,10},{10,14},{3,7},{... | collective-permute-start | bytes 73736 | tf_op jit(solution)/shard_map/ppermute | solution.py:19
  108.0 13.6 %collective-permute-start.8 = (f32[3,16,4,1]{3,1,2,0:T(8,128)S(1)}, f32[3,16,4,1]{3,1,2,0:T(8,128)S(1)}, u32[]{:S(2)}, u32[]{:S(2)}) collective-permute-start(f32[3,16,4,1]{3,1,2,0:T(8,128)S(1)} %get-tuple-element.936), channel_id=1, source_target_pairs={{0,2},{1,3},{4,6},{5,7},{8,10},{9,11},{12,14},{13,15},{16,18},{17,... | collective-permute-start | bytes 2312 | tf_op jit(solution)/shard_map/ppermute | solution.py:19
  109.7 13.3 %collective-permute-start.9 = (f32[3,16,4,1]{3,1,2,0:T(8,128)S(1)}, f32[3,16,4,1]{3,1,2,0:T(8,128)S(1)}, u32[]{:S(2)}, u32[]{:S(2)}) collective-permute-start(f32[3,16,4,1]{3,1,2,0:T(8,128)S(1)} %get-tuple-element.937), channel_id=1, source_target_pairs={{2,0},{3,1},{6,4},{7,5},{10,8},{11,9},{14,12},{15,13},{18,16},{19,... | collective-permute-start | bytes 2312 | tf_op jit(solution)/shard_map/ppermute | solution.py:20
  111.0 16.7 %collective-permute-start.32 = (f32[3,16,4,1]{3,1,2,0:T(8,128)S(1)}, f32[3,16,4,1]{3,1,2,0:T(8,128)S(1)}, u32[]{:S(2)}, u32[]{:S(2)}) collective-permute-start(f32[3,16,4,1]{3,1,2,0:T(8,128)S(1)} %get-tuple-element.948), channel_id=1, source_target_pairs={{0,2},{1,3},{4,6},{5,7},{8,10},{9,11},{12,14},{13,15},{16,18},{17,... | collective-permute-start | bytes 2312 | tf_op jit(solution)/shard_map/ppermute | solution.py:19
  115.6 13.4 %collective-permute-start.33 = (f32[3,16,4,1]{3,1,2,0:T(8,128)S(1)}, f32[3,16,4,1]{3,1,2,0:T(8,128)S(1)}, u32[]{:S(2)}, u32[]{:S(2)}) collective-permute-start(f32[3,16,4,1]{3,1,2,0:T(8,128)S(1)} %get-tuple-element.949), channel_id=1, source_target_pairs={{2,0},{3,1},{6,4},{7,5},{10,8},{11,9},{14,12},{15,13},{18,16},{19,... | collective-permute-start | bytes 2312 | tf_op jit(solution)/shard_map/ppermute | solution.py:20
  117.0 12.3 %collective-permute-start.56 = (f32[3,16,4,1]{3,1,2,0:T(8,128)S(1)}, f32[3,16,4,1]{3,1,2,0:T(8,128)S(1)}, u32[]{:S(2)}, u32[]{:S(2)}) collective-permute-start(f32[3,16,4,1]{3,1,2,0:T(8,128)S(1)} %get-tuple-element.952), channel_id=1, source_target_pairs={{0,2},{1,3},{4,6},{5,7},{8,10},{9,11},{12,14},{13,15},{16,18},{17,... | collective-permute-start | bytes 2312 | tf_op jit(solution)/shard_map/ppermute | solution.py:19
  136.1 13.7 %collective-permute-start.11 = (f32[3,1,4,130]{3,1,2,0:T(1,128)S(1)}, f32[3,1,4,130]{3,1,2,0:T(1,128)S(1)}, u32[]{:S(2)}, u32[]{:S(2)}) collective-permute-start(f32[3,1,4,130]{3,1,2,0:T(1,128)S(1)} %get-tuple-element.801), channel_id=1, source_target_pairs={{0,1},{2,3},{4,5},{6,7},{8,9},{10,11},{12,13},{14,15},{16,17},{18,... | collective-permute-start | bytes 18728 | tf_op jit(solution)/shard_map/ppermute | solution.py:19
  140.8 13.4 %collective-permute-start.35 = (f32[3,1,4,130]{3,1,2,0:T(1,128)S(1)}, f32[3,1,4,130]{3,1,2,0:T(1,128)S(1)}, u32[]{:S(2)}, u32[]{:S(2)}) collective-permute-start(f32[3,1,4,130]{3,1,2,0:T(1,128)S(1)} %get-tuple-element.805), channel_id=1, source_target_pairs={{0,1},{2,3},{4,5},{6,7},{8,9},{10,11},{12,13},{14,15},{16,17},{18,... | collective-permute-start | bytes 18728 | tf_op jit(solution)/shard_map/ppermute | solution.py:19
  158.1 15.8 %collective-permute-start.14 = (f32[3,16,128]{2,1,0:T(8,128)S(1)}, f32[3,16,128]{2,1,0:T(8,128)S(1)}, u32[]{:S(2)}, u32[]{:S(2)}) collective-permute-start(f32[3,16,128]{2,1,0:T(8,128)S(1)} %get-tuple-element.797), channel_id=1, source_target_pairs={{4,0},{8,4},{12,8},{5,1},{9,5},{13,9},{6,2},{10,6},{14,10},{7,3},{... | collective-permute-start | bytes 73736 | tf_op jit(solution)/shard_map/ppermute | solution.py:28
  159.4 14.3 %collective-permute-start.12 = (f32[3,2,128]{2,1,0:T(2,128)S(1)}, f32[3,2,128]{2,1,0:T(2,128)S(1)}, u32[]{:S(2)}, u32[]{:S(2)}) collective-permute-start(f32[3,2,128]{2,1,0:T(2,128)S(1)} %bitcast.1244), channel_id=1, source_target_pairs={{1,0},{3,2},{5,4},{7,6},{9,8},{11,10},{13,12},{15,14},{17,16},{19,... | collective-permute-start | bytes 9224 | tf_op jit(solution)/shard_map/ppermute | solution.py:28
  160.7 12.9 %collective-permute-start.17 = (f32[3,16,2]{1,2,0:T(2,128)S(1)}, f32[3,16,2]{1,2,0:T(2,128)S(1)}, u32[]{:S(2)}, u32[]{:S(2)}) collective-permute-start(f32[3,16,2]{1,2,0:T(2,128)S(1)} %get-tuple-element.662), channel_id=1, source_target_pairs={{0,2},{1,3},{4,6},{5,7},{8,10},{9,11},{12,14},{13,15},{16,18},{17,... | collective-permute-start | bytes 1160 | tf_op jit(solution)/shard_map/ppermute | solution.py:28
  177.0 16.3 %collective-permute-start.18 = (f32[3,2,128]{2,1,0:T(2,128)S(1)}, f32[3,2,128]{2,1,0:T(2,128)S(1)}, u32[]{:S(2)}, u32[]{:S(2)}) collective-permute-start(f32[3,2,128]{2,1,0:T(2,128)S(1)} %bitcast.1241), channel_id=1, source_target_pairs={{1,0},{3,2},{5,4},{7,6},{9,8},{11,10},{13,12},{15,14},{17,16},{19,... | collective-permute-start | bytes 9224 | tf_op jit(solution)/shard_map/ppermute | solution.py:28
  179.7 13.7 %collective-permute-start.20 = (f32[3,16,128]{2,1,0:T(8,128)S(1)}, f32[3,16,128]{2,1,0:T(8,128)S(1)}, u32[]{:S(2)}, u32[]{:S(2)}) collective-permute-start(f32[3,16,128]{2,1,0:T(8,128)S(1)} %get-tuple-element.792), channel_id=1, source_target_pairs={{4,0},{8,4},{12,8},{5,1},{9,5},{13,9},{6,2},{10,6},{14,10},{7,3},{... | collective-permute-start | bytes 73736 | tf_op jit(solution)/shard_map/ppermute | solution.py:28
  181.1 12.0 %collective-permute-start.23 = (f32[3,16,2]{1,2,0:T(2,128)S(1)}, f32[3,16,2]{1,2,0:T(2,128)S(1)}, u32[]{:S(2)}, u32[]{:S(2)}) collective-permute-start(f32[3,16,2]{1,2,0:T(2,128)S(1)} %get-tuple-element.660), channel_id=1, source_target_pairs={{0,2},{1,3},{4,6},{5,7},{8,10},{9,11},{12,14},{13,15},{16,18},{17,... | collective-permute-start | bytes 1160 | tf_op jit(solution)/shard_map/ppermute | solution.py:28
  196.4 16.7 %collective-permute-start.36 = (f32[3,2,128]{2,1,0:T(2,128)S(1)}, f32[3,2,128]{2,1,0:T(2,128)S(1)}, u32[]{:S(2)}, u32[]{:S(2)}) collective-permute-start(f32[3,2,128]{2,1,0:T(2,128)S(1)} %bitcast.1268), channel_id=1, source_target_pairs={{1,0},{3,2},{5,4},{7,6},{9,8},{11,10},{13,12},{15,14},{17,16},{19,... | collective-permute-start | bytes 9224 | tf_op jit(solution)/shard_map/ppermute | solution.py:28
  199.3 13.9 %collective-permute-start.37 = (f32[3,2,128]{2,1,0:T(2,128)S(1)}, f32[3,2,128]{2,1,0:T(2,128)S(1)}, u32[]{:S(2)}, u32[]{:S(2)}) collective-permute-start(f32[3,2,128]{2,1,0:T(2,128)S(1)} %bitcast.1271), channel_id=1, source_target_pairs={{0,1},{2,3},{4,5},{6,7},{8,9},{10,11},{12,13},{14,15},{16,17},{18,... | collective-permute-start | bytes 9224 | tf_op jit(solution)/shard_map/ppermute | solution.py:28
  216.3 16.3 %collective-permute-start.42 = (f32[3,2,128]{2,1,0:T(2,128)S(1)}, f32[3,2,128]{2,1,0:T(2,128)S(1)}, u32[]{:S(2)}, u32[]{:S(2)}) collective-permute-start(f32[3,2,128]{2,1,0:T(2,128)S(1)} %bitcast.1242), channel_id=1, source_target_pairs={{1,0},{3,2},{5,4},{7,6},{9,8},{11,10},{13,12},{15,14},{17,16},{19,... | collective-permute-start | bytes 9224 | tf_op jit(solution)/shard_map/ppermute | solution.py:28
  219.0 13.7 %collective-permute-start.44 = (f32[3,16,128]{2,1,0:T(8,128)S(1)}, f32[3,16,128]{2,1,0:T(8,128)S(1)}, u32[]{:S(2)}, u32[]{:S(2)}) collective-permute-start(f32[3,16,128]{2,1,0:T(8,128)S(1)} %get-tuple-element.781), channel_id=1, source_target_pairs={{4,0},{8,4},{12,8},{5,1},{9,5},{13,9},{6,2},{10,6},{14,10},{7,3},{... | collective-permute-start | bytes 73736 | tf_op jit(solution)/shard_map/ppermute | solution.py:28
  235.7 16.7 %collective-permute-start.60 = (f32[3,2,128]{2,1,0:T(2,128)S(1)}, f32[3,2,128]{2,1,0:T(2,128)S(1)}, u32[]{:S(2)}, u32[]{:S(2)}) collective-permute-start(f32[3,2,128]{2,1,0:T(2,128)S(1)} %bitcast.1269), channel_id=1, source_target_pairs={{1,0},{3,2},{5,4},{7,6},{9,8},{11,10},{13,12},{15,14},{17,16},{19,... | collective-permute-start | bytes 9224 | tf_op jit(solution)/shard_map/ppermute | solution.py:28
  238.6 13.9 %collective-permute-start.61 = (f32[3,2,128]{2,1,0:T(2,128)S(1)}, f32[3,2,128]{2,1,0:T(2,128)S(1)}, u32[]{:S(2)}, u32[]{:S(2)}) collective-permute-start(f32[3,2,128]{2,1,0:T(2,128)S(1)} %bitcast.1272), channel_id=1, source_target_pairs={{0,1},{2,3},{4,5},{6,7},{8,9},{10,11},{12,13},{14,15},{16,17},{18,... | collective-permute-start | bytes 9224 | tf_op jit(solution)/shard_map/ppermute | solution.py:28
  255.5 16.3 %collective-permute-start.66 = (f32[3,2,128]{2,1,0:T(2,128)S(1)}, f32[3,2,128]{2,1,0:T(2,128)S(1)}, u32[]{:S(2)}, u32[]{:S(2)}) collective-permute-start(f32[3,2,128]{2,1,0:T(2,128)S(1)} %bitcast.1243), channel_id=1, source_target_pairs={{1,0},{3,2},{5,4},{7,6},{9,8},{11,10},{13,12},{15,14},{17,16},{19,... | collective-permute-start | bytes 9224 | tf_op jit(solution)/shard_map/ppermute | solution.py:28
  258.3 13.7 %collective-permute-start.68 = (f32[3,16,128]{2,1,0:T(8,128)S(1)}, f32[3,16,128]{2,1,0:T(8,128)S(1)}, u32[]{:S(2)}, u32[]{:S(2)}) collective-permute-start(f32[3,16,128]{2,1,0:T(8,128)S(1)} %get-tuple-element.770), channel_id=1, source_target_pairs={{4,0},{8,4},{12,8},{5,1},{9,5},{13,9},{6,2},{10,6},{14,10},{7,3},{... | collective-permute-start | bytes 73736 | tf_op jit(solution)/shard_map/ppermute | solution.py:28
  275.0 16.7 %collective-permute-start.84 = (f32[3,2,128]{2,1,0:T(2,128)S(1)}, f32[3,2,128]{2,1,0:T(2,128)S(1)}, u32[]{:S(2)}, u32[]{:S(2)}) collective-permute-start(f32[3,2,128]{2,1,0:T(2,128)S(1)} %bitcast.1270), channel_id=1, source_target_pairs={{1,0},{3,2},{5,4},{7,6},{9,8},{11,10},{13,12},{15,14},{17,16},{19,... | collective-permute-start | bytes 9224 | tf_op jit(solution)/shard_map/ppermute | solution.py:28
  277.9 13.9 %collective-permute-start.85 = (f32[3,2,128]{2,1,0:T(2,128)S(1)}, f32[3,2,128]{2,1,0:T(2,128)S(1)}, u32[]{:S(2)}, u32[]{:S(2)}) collective-permute-start(f32[3,2,128]{2,1,0:T(2,128)S(1)} %bitcast.1273), channel_id=1, source_target_pairs={{0,1},{2,3},{4,5},{6,7},{8,9},{10,11},{12,13},{14,15},{16,17},{18,... | collective-permute-start | bytes 9224 | tf_op jit(solution)/shard_map/ppermute | solution.py:28
  314.3 15.7 %collective-permute-start.90 = (f32[3,2,128]{2,1,0:T(2,128)S(1)}, f32[3,2,128]{2,1,0:T(2,128)S(1)}, u32[]{:S(2)}, u32[]{:S(2)}) collective-permute-start(f32[3,2,128]{2,1,0:T(2,128)S(1)} %bitcast.1236), channel_id=1, source_target_pairs={{1,0},{3,2},{5,4},{7,6},{9,8},{11,10},{13,12},{15,14},{17,16},{19,... | collective-permute-start | bytes 9224 | tf_op jit(solution)/shard_map/ppermute | solution.py:28
  317.1 13.1 %collective-permute-start.92 = (f32[3,16,128]{2,1,0:T(8,128)S(1)}, f32[3,16,128]{2,1,0:T(8,128)S(1)}, u32[]{:S(2)}, u32[]{:S(2)}) collective-permute-start(f32[3,16,128]{2,1,0:T(8,128)S(1)} %get-tuple-element.759), channel_id=1, source_target_pairs={{4,0},{8,4},{12,8},{5,1},{9,5},{13,9},{6,2},{10,6},{14,10},{7,3},{... | collective-permute-start | bytes 73736 | tf_op jit(solution)/shard_map/ppermute | solution.py:28
  (53 other events, 427.7 us)
